TPU v7x, 32 devices: a whole 2x2x4 slice. The times are simulated.
32 devices in a mesh: gx: 4 (over x, core), gy: 2 (over y), gz: 4 (over z).
Axes of the slice: x: 2, y: 2, z: 4, core: 2. Of those that a mesh axis runs over, the one named last changes fastest.
Arguments:
- displace: float32 [3, 8, 16, 512], P(None, 'gx', 'gy', 'gz'), may hold values from -0.15 to 0.15
- occupied: int32 [8, 16, 512], P('gx', 'gy', 'gz'), may hold values from 0 to 1, as said below
- strength: float32 [8, 16, 512], P('gx', 'gy', 'gz'), may hold values from 0.5 to 2
Outputs:
- force: float32 [3, 8, 16, 512], P(None, 'gx', 'gy', 'gz')
- energy: float32 [8, 16, 512], P('gx', 'gy', 'gz')
Inputs may be any that keep to these rules, and one draw needn't show every extreme that they name: `occupied`: 0 for a vacancy, 1 for an atom; the share of vacancies differs from domain to domain.
All inputs are finite; a program needn't handle non-finite values.
Results may differ from a plain program's by a relative error of at most 0.00017.
Values sent between devices are 32-bit elements; how exact they have to be, the bound alone decides.
A program may use at most 64 MiB of HBM per device.

v0:
```python
import functools

import jax
import jax.numpy as jnp
from jax import lax
from jax.experimental import pallas as pl
from jax.experimental.pallas import tpu as pltpu
from jax.sharding import PartitionSpec as P

ITERS = 3
RADIUS_SQ = 4.84
STEP = 0.02
AXES = ("gx", "gy", "gz")
MESH = pl.DeviceIdType.MESH
LANES = 128
PLANE = [(dx, dy) for dx in (-1, 0, 1) for dy in (-1, 0, 1)]
NEAR = sorted(
    ((dx, dy, dz) for dx, dy in PLANE for dz in (-1, 0, 1) if (dx, dy, dz) != (0, 0, 0)),
    key=lambda o: (-sum(abs(a) for a in o), o),
)


def minus(o):
    return tuple(-a for a in o)


def up(rows):
    return -(-rows // 8) * 8


def kernel(sizes, counts, disp_hbm, occ_hbm, str_hbm, force_ref, energy_ref,
           xs, ys, zs, xl, yl, zl, stage, near, cols, slopes, disp_ref, occ_ref, str_ref,
           zero, zero_row, sink_x, sink_y, sink_z, tally, send_sem, recv_sem, load_sem):
    cx, cy, cz = sizes
    pitch = cy + 4
    group = LANES // 4
    xu, yu = 3 * cx * cy, 3 * cx * 2
    xpanel, ypanel = xu, yu
    xw, yw = up(xu + 2), up(yu + 2)
    x_rows = (xs.shape[1], xw)
    y_rows = (ys.shape[2], yw)

    loads = [pltpu.make_async_copy(disp_hbm, disp_ref, load_sem.at[0]),
             pltpu.make_async_copy(occ_hbm, occ_ref, load_sem.at[1]),
             pltpu.make_async_copy(str_hbm, str_ref, load_sem.at[2])]
    for load in loads:
        load.start()

    me = [lax.axis_index(axis) for axis in AXES]
    there = [[None if s == 0 else (m + s >= 0) & (m + s < n) for s in (-1, 0, 1)]
             for m, n in zip(me, counts)]

    def exists(o):
        tests = [there[a][o[a] + 1] for a in range(3) if o[a] != 0]
        return functools.reduce(lambda p, q: p & q, tests)

    def target(o):
        return {AXES[a]: me[a] + o[a] for a in range(3)}

    barrier = pltpu.get_barrier_semaphore()
    for o in NEAR:
        @pl.when(exists(o))
        def _(o=o):
            pl.semaphore_signal(barrier, inc=1, device_id=target(o), device_id_type=MESH)
    spans = [1 + (m > 0).astype(jnp.int32) + (m < n - 1).astype(jnp.int32)
             for m, n in zip(me, counts)]

    def ends(t, o):
        back = minus(o)
        if o[2] != 0:
            side = 0 if o[2] == 1 else 1
            src = zs.at[t, side]
            dst = zl.at[t, PLANE.index(back[:2]), side]
        elif o[1] != 0:
            rows = y_rows[0] if t == 0 else y_rows[1]
            side = 0 if o[1] == 1 else 1
            src = ys.at[t, side, pl.ds(0, rows)]
            dst = yl.at[t, back[0] + 1, side, pl.ds(0, rows)]
        else:
            rows = x_rows[0] if t == 0 else x_rows[1]
            src = xs.at[t, pl.ds(0, rows)]
            dst = xl.at[t, 0 if o[0] == 1 else 1, pl.ds(0, rows)]
        return pltpu.make_async_remote_copy(
            src_ref=src, dst_ref=dst, send_sem=send_sem,
            recv_sem=recv_sem.at[t % 2], device_id=target(o), device_id_type=MESH)

    def fill(t, o):
        if o[2] != 0:
            j, side = PLANE.index(o[:2]), 0 if o[2] == -1 else 1
            src, spot, sink = zero_row, zl.at[t, j, side], sink_z.at[j, side]
        elif o[1] != 0:
            rows = pl.ds(0, y_rows[0] if t == 0 else y_rows[1])
            side = 0 if o[1] == -1 else 1
            src, spot = zero.at[rows], yl.at[t, o[0] + 1, side, rows]
            sink = sink_y.at[o[0] + 1, side, rows]
        else:
            rows = pl.ds(0, x_rows[0] if t == 0 else x_rows[1])
            side = 0 if o[0] == -1 else 1
            src, spot, sink = zero.at[rows], xl.at[t, side, rows], sink_x.at[side, rows]
        pltpu.make_async_copy(src, spot, recv_sem.at[t % 2]).start()
        pltpu.make_async_copy(src, sink, send_sem).start()

    zero[...] = jnp.zeros(zero.shape, jnp.float32)
    zero_row[...] = jnp.zeros(zero_row.shape, jnp.float32)
    stage[...] = jnp.zeros(stage.shape, jnp.float32)
    near[...] = jnp.zeros(near.shape, jnp.float32)
    cols[...] = jnp.zeros(cols.shape, jnp.float32)

    for load in loads:
        load.wait()
    mine = [[disp_ref[q, x] for x in range(cx)] for q in range(3)]
    mine.append([occ_ref[x].astype(jnp.float32) * str_ref[x] for x in range(cx)])

    lane = lax.broadcasted_iota(jnp.int32, (8, LANES), 1)
    sub = lax.broadcasted_iota(jnp.int32, (8, LANES), 0)
    in_group = lax.rem(lax.rem(lane, group), pitch)
    depth = (lax.rem(sub, 4) - 1).astype(jnp.float32)
    middle = lax.rem(sub, 4) == 1
    hollow = lax.rem(sub, 4) == 3

    def moved(value, amount, axis=1):
        amount %= value.shape[axis]
        return value if amount == 0 else pltpu.roll(value, amount, axis)

    for t in range(ITERS):
        last = t == ITERS - 1
        for q in range(4):
            for x in range(cx):
                if q < 3 or t == 0:
                    stage[q * group + x * pitch + 2:q * group + x * pitch + 2 + cy] = mine[q][x]
        flipped = jnp.transpose(stage[...])
        head, tail = flipped[0:2], flipped[cz - 2:cz]
        first, final = flipped[0:1], flipped[cz - 1:cz]
        zs[t, 0] = tail
        zs[t, 1] = head
        for side in range(2):
            for q in range(4):
                if q == 3 and t > 0:
                    continue
                for x in range(cx):
                    base = (q * cx + x) * 2 if q < 3 else yw + x * 2
                    piece = mine[q][x]
                    ys[t, side, base:base + 2] = piece[cy - 2:cy] if side == 0 else piece[0:2]
            ys[t, side, ypanel:ypanel + 1] = first
            ys[t, side, ypanel + 1:ypanel + 2] = final
        for q in range(4):
            if q == 3 and t > 0:
                continue
            for x in range(cx):
                base = (q * cx + x) * cy if q < 3 else xw + x * cy
                xs[t, base:base + cy] = mine[q][x]
        xs[t, xpanel:xpanel + 1] = first
        xs[t, xpanel + 1:xpanel + 2] = final

        if t == 0:
            pl.semaphore_wait(barrier, spans[0] * spans[1] * spans[2] - 1)
        for o in NEAR:
            @pl.when(exists(o))
            def _(o=o):
                ends(t, o).start()

            @pl.when(jnp.logical_not(exists(o)))
            def _(o=o):
                fill(t, o)
        pick = 0 if t == 0 else 1
        bytes_of = tally.at[pl.ds(0, (2 * x_rows[pick] + 6 * y_rows[pick] + 36) // 4)]
        pltpu.make_async_copy(bytes_of, bytes_of, recv_sem.at[t % 2]).wait()
        pltpu.make_async_copy(bytes_of, bytes_of, send_sem).wait()

        quantities = range(4) if t == 0 else range(3)
        for q in quantities:
            for dx in (-1, 0, 1):
                for x in range(cx):
                    row = (cx * (dx + 1) + x) * pitch
                    if dx == 0:
                        piece = mine[q][x]
                    else:
                        base = (q * cx + x) * cy if q < 3 else xw + x * cy
                        piece = xl[t, 0 if dx == -1 else 1, base:base + cy]
                    near[1, q, row + 2:row + 2 + cy] = piece
                    base = (q * cx + x) * 2 if q < 3 else yw + x * 2
                    near[1, q, row:row + 2] = yl[t, dx + 1, 0, base:base + 2]
                    near[1, q, row + 2 + cy:row + 4 + cy] = yl[t, dx + 1, 1, base:base + 2]
        for j, (dx, dy) in enumerate(PLANE):
            cols[j, 0:2] = zl[t, j, 0]
            cols[j, 5:7] = zl[t, j, 1]
            if dy != 0:
                a = yl[t, dx + 1, 0 if dy == -1 else 1, ypanel:ypanel + 1]
                b = yl[t, dx + 1, 0 if dy == -1 else 1, ypanel + 1:ypanel + 2]
            elif dx != 0:
                a = xl[t, 0 if dx == -1 else 1, xpanel:xpanel + 1]
                b = xl[t, 0 if dx == -1 else 1, xpanel + 1:xpanel + 2]
            else:
                a, b = first, final
            cols[j, 2:3] = a
            cols[j, 4:5] = b
        joined = []
        for dx in (-1, 0, 1):
            low, mid, high = (cols[PLANE.index((dx, dy))] for dy in (-1, 0, 1))
            joined.append(jnp.where(in_group < 2, moved(low, -cy),
                                    jnp.where(in_group < 2 + cy, mid, moved(high, cy))))
        wide = cx * pitch
        edge = []
        for q in range(4):
            value = jnp.zeros((8, LANES), jnp.float32)
            for i in (2, 1, 0):
                value = jnp.where(lane < wide * (i + 1),
                                  moved(joined[i], wide * i - group * q),
                                  value if i < 2 else 0.0)
            edge.append(value)

        turned = jnp.transpose(jnp.concatenate(edge, axis=0))
        rows = near.shape[2]
        wide_lane = lax.broadcasted_iota(jnp.int32, (rows, LANES), 1)
        for q in quantities:
            here = near[1, q]
            before = turned[0:rows, 8 * q + 1:8 * q + 2]
            after = turned[0:rows, 8 * q + 5:8 * q + 6]
            near[0, q] = jnp.where(wide_lane == 0, before, moved(here, 1))
            near[2, q] = jnp.where(wide_lane == cz - 1, after, moved(here, -1))

        center = [jnp.where(sub < 4, e[1:2], e[5:6]) for e in edge[:3]]
        total = jnp.zeros((8, LANES), jnp.float32)
        for dx, dy in PLANE:
            shift = -(dx * pitch + dy)
            far = [moved(e, shift) for e in edge]
            sx = far[0] - (center[0] - dx)
            sy = far[1] - (center[1] - dy)
            sz = far[2] - (center[2] - depth)
            square = sx * sx + sy * sy + sz * sz
            far_weight = far[3]
            if (dx, dy) == (0, 0):
                square = jnp.where(middle | hollow, 1.0, square)
                far_weight = jnp.where(middle | hollow, 0.0, far_weight)
            distance = square * lax.rsqrt(square)
            inside = 1.0 - square * (1.0 / RADIUS_SQ)
            total = total + far_weight * (jnp.exp(2.0 - 2.0 * distance) * (inside * inside))
        total = total + moved(total, 1, 0) + moved(total, -1, 0)
        edge_slope = jnp.where((edge[3] > 0.0) & middle, -0.5 * lax.rsqrt(1.0 + total), 0.0)
        turned_slope = jnp.transpose(edge_slope)

        begin = pitch + 1
        chunk = 16
        extent = up((cx + 2) * pitch + cy + 3 - begin)
        for start in range(begin, begin + extent, chunk):
            size = min(chunk, begin + extent - start)
            base = [[near[1, q, start:start + size] - s for s in (-1.0, 0.0, 1.0)] for q in range(3)]
            total = jnp.zeros((size, LANES), jnp.float32)
            for dx, dy in PLANE:
                row = start + dx * pitch + dy
                for dz in (-1, 0, 1):
                    if (dx, dy, dz) == (0, 0, 0):
                        continue
                    sx = near[dz + 1, 0, row:row + size] - base[0][dx + 1]
                    sy = near[dz + 1, 1, row:row + size] - base[1][dy + 1]
                    sz = near[dz + 1, 2, row:row + size] - base[2][dz + 1]
                    square = sx * sx + sy * sy + sz * sz
                    distance = square * lax.rsqrt(square)
                    inside = 1.0 - square * (1.0 / RADIUS_SQ)
                    total = total + near[dz + 1, 3, row:row + size] * (
                        jnp.exp(2.0 - 2.0 * distance) * (inside * inside))
            root = lax.rsqrt(1.0 + total)
            slope = jnp.where(near[1, 3, start:start + size] > 0.0, -0.5 * root, 0.0)
            slopes[1, start:start + size] = slope
            tall = lax.broadcasted_iota(jnp.int32, (size, LANES), 1)
            slopes[0, start:start + size] = jnp.where(
                tall == 0, turned_slope[start:start + size, 1:2], moved(slope, 1))
            slopes[2, start:start + size] = jnp.where(
                tall == cz - 1, turned_slope[start:start + size, 5:6], moved(slope, -1))
            if last:
                slopes[3, start:start + size] = (1.0 + total) * root

        for x in range(cx):
            start = (cx + x) * pitch + 2
            here = [mine[q][x] for q in range(3)]
            base = [[h - s for s in (-1.0, 0.0, 1.0)] for h in here]
            weight = mine[3][x]
            slope = slopes[1, start:start + cy]
            force = [jnp.zeros((cy, LANES), jnp.float32) for _ in range(3)]
            pair = jnp.zeros((cy, LANES), jnp.float32)
            for dx, dy in PLANE:
                row = start + dx * pitch + dy
                for dz in (-1, 0, 1):
                    if (dx, dy, dz) == (0, 0, 0):
                        continue
                    sx = near[dz + 1, 0, row:row + cy] - base[0][dx + 1]
                    sy = near[dz + 1, 1, row:row + cy] - base[1][dy + 1]
                    sz = near[dz + 1, 2, row:row + cy] - base[2][dz + 1]
                    far_weight = near[dz + 1, 3, row:row + cy]
                    far_slope = slopes[dz + 1, row:row + cy]
                    square = sx * sx + sy * sy + sz * sz
                    inverse = lax.rsqrt(square)
                    distance = square * inverse
                    inside = 1.0 - square * (1.0 / RADIUS_SQ)
                    cut = inside * inside
                    cut_slope = inside * distance * (-4.0 / RADIUS_SQ)
                    growth = jnp.exp(2.0 - 2.0 * distance)
                    steep = 0.5 * growth * growth
                    coupling = (slope * far_weight + far_slope * weight) * (
                        growth * (cut_slope - 2.0 * cut)) + weight * far_weight * (
                        steep * (cut_slope - 4.0 * cut))
                    scale = coupling * inverse
                    force = [force[0] + scale * sx, force[1] + scale * sy, force[2] + scale * sz]
                    if last:
                        pair = pair + far_weight * (steep * cut)
            if last:
                for q in range(3):
                    force_ref[q, x] = force[q]
                energy_ref[x] = 0.5 * weight * pair - jnp.where(
                    weight > 0.0, slopes[3, start:start + cy], 0.0)
            else:
                for q in range(3):
                    mine[q][x] = here[q] + STEP * force[q]


def solution(mesh):
    counts = tuple(mesh.shape[axis] for axis in AXES)

    def body(displace, occupied, strength):
        sizes = occupied.shape
        cx, cy, cz = sizes
        pitch = cy + 4
        x_rows = up(3 * cx * cy + 2) + up(cx * cy)
        y_rows = up(6 * cx + 2) + up(2 * cx)
        rows = up(2 * (pitch + 1) + up((cx + 2) * pitch + cy + 3 - (pitch + 1)))
        f32 = jnp.float32
        vmem = pl.BlockSpec(memory_space=pltpu.VMEM)
        return pl.pallas_call(
            functools.partial(kernel, sizes, counts),
            out_shape=(pltpu.VMEM((3,) + sizes, f32), pltpu.VMEM(sizes, f32)),
            in_specs=[pl.BlockSpec(memory_space=pl.ANY)] * 3,
            out_specs=(vmem, vmem),
            scratch_shapes=[
                pltpu.VMEM((ITERS, x_rows, LANES), f32),
                pltpu.VMEM((ITERS, 2, y_rows, LANES), f32),
                pltpu.VMEM((ITERS, 2, 2, LANES), f32),
                pltpu.VMEM((ITERS, 2, x_rows, LANES), f32),
                pltpu.VMEM((ITERS, 3, 2, y_rows, LANES), f32),
                pltpu.VMEM((ITERS, 9, 2, 2, LANES), f32),
                pltpu.VMEM((LANES, LANES), f32),
                pltpu.VMEM((3, 4, rows, LANES), f32),
                pltpu.VMEM((9, 8, LANES), f32),
                pltpu.VMEM((4, rows, LANES), f32),
                pltpu.VMEM((3,) + sizes, f32),
                pltpu.VMEM(sizes, jnp.int32),
                pltpu.VMEM(sizes, f32),
                pltpu.VMEM((x_rows, LANES), f32),
                pltpu.VMEM((2, LANES), f32),
                pltpu.VMEM((2, x_rows, LANES), f32),
                pltpu.VMEM((3, 2, y_rows, LANES), f32),
                pltpu.VMEM((9, 2, 2, LANES), f32),
                pltpu.VMEM(((2 * x_rows + 6 * y_rows + 36) // 4, 4, LANES), f32),
                pltpu.SemaphoreType.DMA,
                pltpu.SemaphoreType.DMA((2,)),
                pltpu.SemaphoreType.DMA((3,)),
            ],
            compiler_params=pltpu.CompilerParams(collective_id=0, has_side_effects=True),
        )(displace, occupied, strength)

    in_specs = (P(None, "gx", "gy", "gz"), P("gx", "gy", "gz"), P("gx", "gy", "gz"))
    out_specs = (P(None, "gx", "gy", "gz"), P("gx", "gy", "gz"))
    return jax.shard_map(body, mesh=mesh, in_specs=in_specs, out_specs=out_specs, check_vma=False)
```

profile of v0, /device:TPU:1, one launch (start us, length us, event | category | flops | bytes accessed | tf_op | source)
XLA Modules:
  0.0 20.5 jit_solution(15691228501227334670)
XLA Ops:
  0.6 18.6 %shard_map.50 = (f32[3,2,8,128]{3,2,1,0:T(8,128)S(1)}, f32[2,8,128]{2,1,0:T(8,128)S(1)}) custom-call(f32[3,2,8,128]{3,2,1,0:T(8,128)} %disp_hbm.1, s32[2,8,128]{2,1,0:T(8,128)} %occ_hbm.1, f32[2,8,128]{2,1,0:T(8,128)} %str_hbm.1), custom_call_target="tpu_custom_call" | custom-call | tf_op jit(solution)/shard_map/pallas_call | solution.py:328
  19.3 0.6 %copy.7 = f32[3,2,8,128]{3,2,1,0:T(8,128)} copy(f32[3,2,8,128]{3,2,1,0:T(8,128)S(1)} %get-tuple-element.2) | data formatting | bytes 49152
  19.9 0.6 %copy.8 = f32[2,8,128]{2,1,0:T(8,128)} copy(f32[2,8,128]{2,1,0:T(8,128)S(1)} %get-tuple-element.3) | data formatting | bytes 16384
where the time goes:
time: 20.6 us; the launch traced here: 20.5 us
  Pallas kernels  18.6 us (90%)
  local copies, waits for them, and re-layouts  1.21 us (6%)
  between operations  0.64 us (3%)
    pallas_call x1, Pallas kernels, body(): pl.pallas_call(functools.partial(kernel, sizes, counts), out_shape=(pltpu...  18.6 us
    unnamed x2, local copies, waits for them, and re-layouts  1.21 us

commit v1 on v0

v1 whole, which is shorter than its diff:
```python
import functools
import math

import jax
import jax.numpy as jnp
from jax import lax
from jax.experimental import pallas as pl
from jax.experimental.pallas import tpu as pltpu
from jax.sharding import PartitionSpec as P

ITERS = 3
RADIUS_SQ = 4.84
STEP = 0.02
AXES = ("gx", "gy", "gz")
MESH = pl.DeviceIdType.MESH
LANES = 128
DEEP = 2 * ITERS
PLANE = [(dx, dy) for dx in (-1, 0, 1) for dy in (-1, 0, 1)]
FLAT = sorted(((dx, dy, 0) for dx, dy in PLANE if (dx, dy) != (0, 0)),
              key=lambda o: (-sum(abs(a) for a in o), o))
TALL = sorted(((dx, dy, dz) for dx, dy in PLANE for dz in (-1, 1)),
              key=lambda o: (-sum(abs(a) for a in o), o))
PANELS = TALL + FLAT

RADIUS = math.sqrt(RADIUS_SQ)
UNIT = 1.0 / RADIUS
RATE = -2.0 * RADIUS / math.log(2.0)
SQUARED_E = math.exp(2.0)
PULL = 2.0 / RADIUS
PUSH = 1.0 / RADIUS
FORCE = -2.0 * SQUARED_E * SQUARED_E
PAIR = 0.5 * 0.5 * SQUARED_E * SQUARED_E


def minus(o):
    return tuple(-a for a in o)


def up(rows):
    return -(-rows // 8) * 8


def low(a):
    return 0 if a == -1 else 1


def moved(value, amount, axis=1):
    amount %= value.shape[axis]
    return value if amount == 0 else pltpu.roll(value, amount, axis)


def density_sum(near, here, size):
    base = [[h - s * UNIT for s in (-1.0, 0.0, 1.0)] for h in here]
    total = jnp.zeros((size, LANES), jnp.float32)
    for dx, dy in PLANE:
        for dz in (-1, 0, 1):
            if (dx, dy, dz) == (0, 0, 0):
                continue
            sx = near(dx, dy, dz, 0) - base[0][dx + 1]
            sy = near(dx, dy, dz, 1) - base[1][dy + 1]
            sz = near(dx, dy, dz, 2) - base[2][dz + 1]
            square = sx * sx + sy * sy + sz * sz
            distance = square * lax.rsqrt(square)
            inside = 1.0 - square
            total = total + near(dx, dy, dz, 3) * (
                jnp.exp2(distance * RATE) * (inside * inside))
    return total


def force_sum(near, slope_near, here, slope, size, last):
    base = [[h - s * UNIT for s in (-1.0, 0.0, 1.0)] for h in here]
    force = [jnp.zeros((size, LANES), jnp.float32) for _ in range(3)]
    pair = jnp.zeros((size, LANES), jnp.float32)
    for dx, dy in PLANE:
        for dz in (-1, 0, 1):
            if (dx, dy, dz) == (0, 0, 0):
                continue
            sx = near(dx, dy, dz, 0) - base[0][dx + 1]
            sy = near(dx, dy, dz, 1) - base[1][dy + 1]
            sz = near(dx, dy, dz, 2) - base[2][dz + 1]
            weight = near(dx, dy, dz, 3)
            square = sx * sx + sy * sy + sz * sz
            inverse = lax.rsqrt(square)
            growth = jnp.exp2(square * inverse * RATE)
            inside = 1.0 - square
            steep = PULL + inside * inverse
            both = slope + slope_near(dx, dy, dz)
            cut = growth * inside
            scale = (both * steep + growth * (steep - PUSH)) * cut * weight
            force = [force[0] + scale * sx, force[1] + scale * sy, force[2] + scale * sz]
            if last:
                pair = pair + weight * (cut * cut)
    return force, pair


def kernel(sizes, counts, disp_hbm, occ_hbm, str_hbm, force_ref, energy_ref,
           disp_ref, occ_ref, str_ref, xs, ys, xl, yl, near, slopes, scaled,
           stage, ps, px, pz, sp, sn, ss, sscaled, sroot, xp, xq, final,
           main_send, main_recv, panel_send, panel_recv, strip_send, strip_recv, load_sem, ready):
    cx, cy, cz = sizes
    pitch = cy + 4
    wide = cy + 2 * DEEP
    group = cx * wide
    f32 = jnp.float32

    loads = [pltpu.make_async_copy(disp_hbm, disp_ref, load_sem.at[0]),
             pltpu.make_async_copy(occ_hbm, occ_ref, load_sem.at[1]),
             pltpu.make_async_copy(str_hbm, str_ref, load_sem.at[2])]
    for load in loads:
        load.start()

    me = [lax.axis_index(axis) for axis in AXES]
    there = [[None if s == 0 else (m + s >= 0) & (m + s < n) for s in (-1, 0, 1)]
             for m, n in zip(me, counts)]

    def exists(o):
        tests = [there[a][o[a] + 1] for a in range(3) if o[a] != 0]
        return functools.reduce(lambda p, q: p & q, tests)

    def target(o):
        return {AXES[a]: me[a] + o[a] for a in range(3)}

    ends_z = [(0, 0, -1), (0, 0, 1)]
    barrier = pltpu.get_barrier_semaphore()
    for o in ends_z + FLAT:
        @pl.when(exists(o))
        def _(o=o):
            pl.semaphore_signal(barrier, inc=1, device_id=target(o), device_id_type=MESH)
    spans = [1 + (m > 0).astype(jnp.int32) + (m < n - 1).astype(jnp.int32)
             for m, n in zip(me, counts)]

    for s in (-1, 1):
        @pl.when(jnp.logical_not(there[0][s + 1]))
        def _(s=s):
            xl[:, low(s)] = jnp.zeros(xl.shape[:1] + xl.shape[2:], f32)
            yl[:, s + 1] = jnp.zeros(yl.shape[:1] + yl.shape[2:], f32)
            xq[:, low(s)] = jnp.zeros(xq.shape[:1] + xq.shape[2:], f32)
            px[3 * (s + 1):3 * (s + 1) + 3] = jnp.zeros((3,) + px.shape[1:], f32)
            pz[3 * (s + 1):3 * (s + 1) + 3] = jnp.zeros((3,) + pz.shape[1:], f32)

        @pl.when(jnp.logical_not(there[1][s + 1]))
        def _(s=s):
            yl[:, :, low(s)] = jnp.zeros(yl.shape[:2] + yl.shape[3:], f32)
            for dx in range(3):
                px[3 * dx + s + 1] = jnp.zeros(px.shape[1:], f32)
                pz[3 * dx + s + 1] = jnp.zeros(pz.shape[1:], f32)

        @pl.when(jnp.logical_not(there[2][s + 1]))
        def _(s=s):
            pz[:, low(s)] = jnp.zeros(pz.shape[:1] + pz.shape[2:], f32)

    stage[...] = jnp.zeros(stage.shape, f32)
    near[...] = jnp.zeros(near.shape, f32)
    sn[...] = jnp.zeros(sn.shape, f32)
    ss[...] = jnp.zeros(ss.shape, f32)

    def main_rows(t, face):
        return (4 if t == 0 else 3) * cx * cy if face else up((4 if t == 0 else 3) * cx * 2)

    def main_send_to(t, o):
        back = minus(o)
        rows = pl.ds(0, main_rows(t, o[1] == 0))
        if o[1] == 0:
            src, dst = xs.at[t, rows], xl.at[t, low(back[0]), rows]
        else:
            src, dst = ys.at[t, low(back[1]), rows], yl.at[t, back[0] + 1, low(back[1]), rows]
        return pltpu.make_async_remote_copy(
            src_ref=src, dst_ref=dst, send_sem=main_send.at[t, FLAT.index(o)],
            recv_sem=main_recv.at[t, FLAT.index(back)], device_id=target(o), device_id_type=MESH)

    def main_from(t, o):
        rows = pl.ds(0, main_rows(t, o[1] == 0))
        spot = xl.at[t, low(o[0]), rows] if o[1] == 0 else yl.at[t, o[0] + 1, low(o[1]), rows]
        return pltpu.make_async_remote_copy(
            src_ref=spot, dst_ref=spot, send_sem=main_send.at[t, FLAT.index(o)],
            recv_sem=main_recv.at[t, FLAT.index(o)], device_id=target(o), device_id_type=MESH)

    def panel_spot(o):
        j = PLANE.index(o[:2])
        return px.at[j] if o[2] == 0 else pz.at[j, low(o[2])]

    def panel_to(o):
        back = minus(o)
        rows = pl.ds(0, 32) if o[2] == 0 else pl.ds(8 if o[2] == -1 else 16, 16)
        return pltpu.make_async_remote_copy(
            src_ref=ps.at[back[1] + 1, rows], dst_ref=panel_spot(back),
            send_sem=panel_send.at[PANELS.index(o)], recv_sem=panel_recv.at[PANELS.index(back)],
            device_id=target(o), device_id_type=MESH)

    def panel_from(o):
        return pltpu.make_async_remote_copy(
            src_ref=panel_spot(o), dst_ref=panel_spot(o),
            send_sem=panel_send.at[PANELS.index(o)], recv_sem=panel_recv.at[PANELS.index(o)],
            device_id=target(o), device_id_type=MESH)

    def strip_to(t, o):
        back = minus(o)
        return pltpu.make_async_remote_copy(
            src_ref=xp.at[t], dst_ref=xq.at[t, low(back[0])],
            send_sem=strip_send.at[t, low(o[0])], recv_sem=strip_recv.at[t, low(back[0])],
            device_id=target(o), device_id_type=MESH)

    def strip_from(t, o):
        spot = xq.at[t, low(o[0])]
        return pltpu.make_async_remote_copy(
            src_ref=spot, dst_ref=spot,
            send_sem=strip_send.at[t, low(o[0])], recv_sem=strip_recv.at[t, low(o[0])],
            device_id=target(o), device_id_type=MESH)

    def each(offsets, act):
        for o in offsets:
            @pl.when(exists(o))
            def _(o=o):
                act(o)

    SIDES = [(-1, 0, 0), (1, 0, 0)]

    for load in loads:
        load.wait()
    mine = [[disp_ref[q, x] * UNIT for x in range(cx)] for q in range(3)]
    mine.append([occ_ref[x].astype(f32) * str_ref[x] for x in range(cx)])

    def fill_sends(t):
        for q in range(4 if t == 0 else 3):
            for x in range(cx):
                i = q * cx + x
                xs[t, i * cy:(i + 1) * cy] = mine[q][x]
                ys[t, 0, i * 2:i * 2 + 2] = mine[q][x][cy - 2:cy]
                ys[t, 1, i * 2:i * 2 + 2] = mine[q][x][0:2]

    def put(q, row, piece):
        rows = piece.shape[0]
        near[0, q, row:row + rows] = moved(piece, 1)
        near[1, q, row:row + rows] = piece
        near[2, q, row:row + rows] = moved(piece, -1)

    def put_mine(t):
        for q in range(4 if t == 0 else 3):
            for x in range(cx):
                put(q, (cx + x) * pitch + 2, mine[q][x])

    def put_others(t):
        for q in range(4 if t == 0 else 3):
            for x in range(cx):
                i = q * cx + x
                for dx in (-1, 0, 1):
                    row = (cx * (dx + 1) + x) * pitch
                    if dx != 0:
                        put(q, row + 2, xl[t, low(dx), i * cy:(i + 1) * cy])
                    put(q, row, yl[t, dx + 1, 0, i * 2:i * 2 + 2])
                    put(q, row + 2 + cy, yl[t, dx + 1, 1, i * 2:i * 2 + 2])

    fill_sends(0)
    pl.semaphore_wait(barrier, spans[0] * spans[1] + spans[2] - 2)
    each(FLAT, lambda o: main_send_to(0, o).start())
    each(ends_z, lambda o: pl.semaphore_signal(
        ready, inc=1, device_id=target(o), device_id_type=MESH))

    lane = lax.broadcasted_iota(jnp.int32, (8, LANES), 1)
    half = lax.broadcasted_iota(jnp.int32, (8, LANES), 0) < 4
    column = lax.rem(lane, wide)
    for x in range(cx):
        for q in range(3):
            row = q * group + x * wide + DEEP
            stage[0, row:row + cy] = mine[q][x]
            stage[1, row:row + cy] = mine[3][x]
    turned = jnp.transpose(stage[0])
    heavy = jnp.transpose(stage[1])

    def ends_of(value):
        return (value[0:8], jnp.where(half, value[8:16], value[cz - 16:cz - 8]), value[cz - 8:cz])

    first, middle, end = ends_of(turned)
    load_first, load_middle, load_end = ends_of(heavy)
    load = jnp.where(lane < group, load_first, jnp.where(lane < 2 * group, load_middle, load_end))
    for i, piece in enumerate((middle, first, load, end)):
        ps[1, 8 * i:8 * i + 8] = piece
        ps[0, 8 * i:8 * i + 8] = jnp.where(column < DEEP, moved(piece, -cy), 0.0)
        ps[2, 8 * i:8 * i + 8] = jnp.where(column >= DEEP + cy, moved(piece, cy), 0.0)
    each(FLAT, lambda o: panel_to(o).start())
    pl.semaphore_wait(ready, spans[2] - 1)
    each(TALL, lambda o: panel_to(o).start())

    put_mine(0)

    begin = pitch + 1
    chunk = 16
    extent = up((cx + 2) * pitch + cy + 3 - begin)

    def main_step(t):
        last = t == ITERS - 1
        each(FLAT, lambda o: main_from(t, o).wait_recv())
        put_others(t)
        if t == 0:
            weight = near[1, 3, begin:begin + extent]
            scaled[begin:begin + extent] = jnp.where(
                weight > 0.0, (-0.5 / SQUARED_E) / jnp.where(weight > 0.0, weight, 1.0), 0.0)
        for start in range(begin, begin + extent, chunk):
            size = min(chunk, begin + extent - start)

            def around(dx, dy, dz, q, start=start, size=size):
                row = start + dx * pitch + dy
                return near[dz + 1, q, row:row + size]

            total = 1.0 + SQUARED_E * density_sum(
                around, [near[1, q, start:start + size] for q in range(3)], size)
            root = lax.rsqrt(total)
            slope = scaled[start:start + size] * root
            slopes[0, start:start + size] = moved(slope, 1)
            slopes[1, start:start + size] = slope
            slopes[2, start:start + size] = moved(slope, -1)
            if last:
                slopes[3, start:start + size] = total * root
        for x in range(cx):
            start = (cx + x) * pitch + 2

            def around(dx, dy, dz, q, start=start):
                row = start + dx * pitch + dy
                return near[dz + 1, q, row:row + cy]

            def slope_around(dx, dy, dz, start=start):
                row = start + dx * pitch + dy
                return slopes[dz + 1, row:row + cy]

            here = [mine[q][x] for q in range(3)]
            force, pair = force_sum(around, slope_around, here, slopes[1, start:start + cy], cy, last)
            weight = mine[3][x]
            if last:
                for q in range(3):
                    force_ref[q, x] = (weight * FORCE) * force[q]
                energy_ref[x] = (weight * PAIR) * pair - jnp.where(
                    weight > 0.0, slopes[3, start:start + cy], 0.0)
            else:
                for q in range(3):
                    mine[q][x] = here[q] + (weight * (FORCE * STEP * UNIT)) * force[q]
        if not last:
            fill_sends(t + 1)
            each(FLAT, lambda o: main_send_to(t + 1, o).start())
            put_mine(t + 1)

    def spread(parts, at):
        found = [moved(parts[i], group * (i - at)) for i in range(3)]
        return jnp.where(lane < group, found[0], jnp.where(
            lane < 2 * group, found[1], jnp.where(lane < 3 * group, found[2], 0.0)))

    def put_strip(q, row, value):
        for j, (dx, dy) in enumerate(PLANE):
            sp[j, q, row:row + 8] = moved(value, -(dx * wide + dy))

    def strip_step(t):
        last = t == ITERS - 1
        if t == 0:
            each(PANELS, lambda o: panel_from(o).wait_recv())

            def flat(rows):
                return [sum(ps[1, rows:rows + 8] if (dx, dy) == (0, 0)
                            else px[PLANE.index((dx, dy)), rows:rows + 8] for dy in (-1, 0, 1))
                        for dx in (-1, 0, 1)]

            def tall(side, rows):
                return [sum(pz[PLANE.index((dx, dy)), side, rows:rows + 8] for dy in (-1, 0, 1))
                        for dx in (-1, 0, 1)]

            blocks = [tall(0, 8), flat(8), flat(0), flat(24), tall(1, 0)]
            for b, parts in enumerate(blocks):
                for q in range(3):
                    put_strip(q, 8 * b, spread(parts, q))
            loads_at = flat(16)
            for b, (parts, at) in enumerate(((tall(0, 0), 2), (loads_at, 0), (loads_at, 1),
                                             (loads_at, 2), (tall(1, 8), 0))):
                weight = spread(parts, at)
                put_strip(3, 8 * b, weight)
                sscaled[8 * b:8 * b + 8] = jnp.where(
                    weight > 0.0, (-0.5 / SQUARED_E) / jnp.where(weight > 0.0, weight, 1.0), 0.0)
        else:
            each(SIDES, lambda o: strip_from(t - 1, o).wait_recv())
            for b in range(4):
                for q in range(3):
                    under = moved(xq[t - 1, 0, 8 * b:8 * b + 8], -group * q)
                    over = moved(xq[t - 1, 1, 8 * b:8 * b + 8], group * (2 - q))
                    put_strip(q, 4 + 8 * b, jnp.where(lane < group, under, jnp.where(
                        lane < 2 * group, sn[q, 4 + 8 * b:12 + 8 * b],
                        jnp.where(lane < 3 * group, over, 0.0))))

        reach = 2 * (ITERS - 1 - t)
        starts = []
        for base in (8, 32 - DEEP):
            starts += sorted({base - reach - 1, base + DEEP + reach + 1 - 8})
        for row in starts:
            def around(dx, dy, dz, q, row=row):
                return sp[PLANE.index((dx, dy)), q, row + dz:row + dz + 8]

            total = 1.0 + SQUARED_E * density_sum(
                around, [sp[4, q, row:row + 8] for q in range(3)], 8)
            root = lax.rsqrt(total)
            slope = sscaled[row:row + 8] * root
            for j, (dx, dy) in enumerate(PLANE):
                ss[j, row:row + 8] = moved(slope, -(dx * wide + dy))
            if last:
                sroot[row:row + 8] = total * root
        starts = [8, 24]
        if not last:
            starts = []
            for base in (8, 32 - DEEP):
                starts += sorted({base - reach, base + DEEP + reach - 8})
        results = []
        for row in starts:
            def around(dx, dy, dz, q, row=row):
                return sp[PLANE.index((dx, dy)), q, row + dz:row + dz + 8]

            def slope_around(dx, dy, dz, row=row):
                return ss[PLANE.index((dx, dy)), row + dz:row + dz + 8]

            here = [sp[4, q, row:row + 8] for q in range(3)]
            force, pair = force_sum(around, slope_around, here, ss[4, row:row + 8], 8, last)
            weight = sp[4, 3, row:row + 8]
            if last:
                energy = (weight * PAIR) * pair - jnp.where(
                    weight > 0.0, sroot[row:row + 8], 0.0)
                results.append([(weight * FORCE) * f for f in force] + [energy])
            else:
                for q in range(3):
                    sn[q, row:row + 8] = here[q] + (weight * (FORCE * STEP * UNIT)) * force[q]
        if not last:
            for b in range(4):
                new = [moved(sn[q, 4 + 8 * b:12 + 8 * b], group * (q - 1)) for q in range(3)]
                xp[t, 8 * b:8 * b + 8] = jnp.where(
                    lane < group, new[0], jnp.where(lane < 2 * group, new[1], new[2]))
            each(SIDES, lambda o: strip_to(t, o).start())
            return
        rows = []
        for q in range(4):
            rows += [results[1][q], results[0][q]]
        rows.append(jnp.zeros((LANES - 64, LANES), f32))
        final[...] = jnp.transpose(jnp.concatenate(rows, axis=0))
        outer = (lane < DEEP) | (lane >= cz - DEEP)
        for q in range(4):
            for x in range(cx):
                start = group + x * wide + DEEP
                piece = moved(final[start:start + cy], cz - 8 - 16 * q)
                spot = force_ref.at[q, x] if q < 3 else energy_ref.at[x]
                spot[...] = jnp.where(outer, piece, spot[...])

    for t in range(ITERS):
        main_step(t)
        strip_step(t)
        if t == 0:
            each(PANELS, lambda o: panel_to(o).wait_send())
            each(FLAT, lambda o: main_send_to(0, o).wait_send())
        else:
            each(FLAT, lambda o: main_send_to(t, o).wait_send())
            each(SIDES, lambda o: strip_to(t - 1, o).wait_send())


def solution(mesh):
    counts = tuple(mesh.shape[axis] for axis in AXES)

    def body(displace, occupied, strength):
        sizes = occupied.shape
        cx, cy, cz = sizes
        assert cx == 2 and cy == 8 and cz == LANES
        pitch = cy + 4
        rows = up(2 * (pitch + 1) + up((cx + 2) * pitch + cy + 3 - (pitch + 1)))
        f32 = jnp.float32
        vmem = pl.BlockSpec(memory_space=pltpu.VMEM)
        return pl.pallas_call(
            functools.partial(kernel, sizes, counts),
            out_shape=(pltpu.VMEM((3,) + sizes, f32), pltpu.VMEM(sizes, f32)),
            in_specs=[pl.BlockSpec(memory_space=pl.ANY)] * 3,
            out_specs=(vmem, vmem),
            scratch_shapes=[
                pltpu.VMEM((3,) + sizes, f32),
                pltpu.VMEM(sizes, jnp.int32),
                pltpu.VMEM(sizes, f32),
                pltpu.VMEM((ITERS, 4 * cx * cy, LANES), f32),
                pltpu.VMEM((ITERS, 2, up(8 * cx), LANES), f32),
                pltpu.VMEM((ITERS, 2, 4 * cx * cy, LANES), f32),
                pltpu.VMEM((ITERS, 3, 2, up(8 * cx), LANES), f32),
                pltpu.VMEM((3, 4, rows, LANES), f32),
                pltpu.VMEM((4, rows, LANES), f32),
                pltpu.VMEM((rows, LANES), f32),
                pltpu.VMEM((2, LANES, LANES), f32),
                pltpu.VMEM((3, 32, LANES), f32),
                pltpu.VMEM((9, 32, LANES), f32),
                pltpu.VMEM((9, 2, 16, LANES), f32),
                pltpu.VMEM((9, 4, 40, LANES), f32),
                pltpu.VMEM((3, 40, LANES), f32),
                pltpu.VMEM((9, 40, LANES), f32),
                pltpu.VMEM((40, LANES), f32),
                pltpu.VMEM((40, LANES), f32),
                pltpu.VMEM((ITERS - 1, 32, LANES), f32),
                pltpu.VMEM((ITERS - 1, 2, 32, LANES), f32),
                pltpu.VMEM((LANES, LANES), f32),
                pltpu.SemaphoreType.DMA((ITERS, len(FLAT))),
                pltpu.SemaphoreType.DMA((ITERS, len(FLAT))),
                pltpu.SemaphoreType.DMA((len(PANELS),)),
                pltpu.SemaphoreType.DMA((len(PANELS),)),
                pltpu.SemaphoreType.DMA((ITERS - 1, 2)),
                pltpu.SemaphoreType.DMA((ITERS - 1, 2)),
                pltpu.SemaphoreType.DMA((3,)),
                pltpu.SemaphoreType.REGULAR,
            ],
            compiler_params=pltpu.CompilerParams(collective_id=0, has_side_effects=True),
        )(displace, occupied, strength)

    in_specs = (P(None, "gx", "gy", "gz"), P("gx", "gy", "gz"), P("gx", "gy", "gz"))
    out_specs = (P(None, "gx", "gy", "gz"), P("gx", "gy", "gz"))
    return jax.shard_map(body, mesh=mesh, in_specs=in_specs, out_specs=out_specs, check_vma=False)
```

time: 20.6 us -> 19.4 us (0.942)
  Pallas kernels: 18.6 us -> 17.4 us
    pallas_call x1, Pallas kernels: 18.6 us -> 17.4 us  [body(): pl.pallas_call(functools.partial(kernel, sizes, counts), out_shape=(pltpu...]
where the time goes in v1:
time: 19.4 us; the launch traced here: 19.2 us
  Pallas kernels  17.4 us (90%)
  local copies, waits for them, and re-layouts  1.21 us (6%)
  between operations  0.64 us (3%)
    pallas_call x1, Pallas kernels, body(): pl.pallas_call(functools.partial(kernel, sizes, counts), out_shape=(pltpu...  17.4 us
    unnamed x2, local copies, waits for them, and re-layouts  1.21 us

profile of v1, /device:TPU:1, one launch (start us, length us, event | category | flops | bytes accessed | tf_op | source)
XLA Modules:
  0.0 19.2 jit_solution(4802117940482793616)
XLA Ops:
  0.6 17.4 %shard_map.50 = (f32[3,2,8,128]{3,2,1,0:T(8,128)S(1)}, f32[2,8,128]{2,1,0:T(8,128)S(1)}) custom-call(f32[3,2,8,128]{3,2,1,0:T(8,128)} %disp_hbm.1, s32[2,8,128]{2,1,0:T(8,128)} %occ_hbm.1, f32[2,8,128]{2,1,0:T(8,128)} %str_hbm.1), custom_call_target="tpu_custom_call" | custom-call | tf_op jit(solution)/shard_map/pallas_call | solution.py:466
  18.0 0.6 %copy.7 = f32[3,2,8,128]{3,2,1,0:T(8,128)} copy(f32[3,2,8,128]{3,2,1,0:T(8,128)S(1)} %get-tuple-element.2) | data formatting | bytes 49152
  18.6 0.6 %copy.8 = f32[2,8,128]{2,1,0:T(8,128)} copy(f32[2,8,128]{2,1,0:T(8,128)S(1)} %get-tuple-element.3) | data formatting | bytes 16384

commit v2 on v1

--- a/solution.py
+++ b/solution.py
@@ -96,7 +96,7 @@
 def kernel(sizes, counts, disp_hbm, occ_hbm, str_hbm, force_ref, energy_ref,
            disp_ref, occ_ref, str_ref, xs, ys, xl, yl, near, slopes, scaled,
            stage, ps, px, pz, sp, sn, ss, sscaled, sroot, xp, xq, final,
-           main_send, main_recv, panel_send, panel_recv, strip_send, strip_recv, load_sem, ready):
+           main_send, main_recv, panel_send, panel_recv, strip_send, strip_recv, load_sem):
     cx, cy, cz = sizes
     pitch = cy + 4
     wide = cy + 2 * DEEP
@@ -120,9 +120,8 @@
     def target(o):
         return {AXES[a]: me[a] + o[a] for a in range(3)}
 
-    ends_z = [(0, 0, -1), (0, 0, 1)]
     barrier = pltpu.get_barrier_semaphore()
-    for o in ends_z + FLAT:
+    for o in PANELS:
         @pl.when(exists(o))
         def _(o=o):
             pl.semaphore_signal(barrier, inc=1, device_id=target(o), device_id_type=MESH)
@@ -251,10 +250,6 @@
                     put(q, row + 2 + cy, yl[t, dx + 1, 1, i * 2:i * 2 + 2])
 
     fill_sends(0)
-    pl.semaphore_wait(barrier, spans[0] * spans[1] + spans[2] - 2)
-    each(FLAT, lambda o: main_send_to(0, o).start())
-    each(ends_z, lambda o: pl.semaphore_signal(
-        ready, inc=1, device_id=target(o), device_id_type=MESH))
 
     lane = lax.broadcasted_iota(jnp.int32, (8, LANES), 1)
     half = lax.broadcasted_iota(jnp.int32, (8, LANES), 0) < 4
@@ -277,11 +272,10 @@
         ps[1, 8 * i:8 * i + 8] = piece
         ps[0, 8 * i:8 * i + 8] = jnp.where(column < DEEP, moved(piece, -cy), 0.0)
         ps[2, 8 * i:8 * i + 8] = jnp.where(column >= DEEP + cy, moved(piece, cy), 0.0)
-    each(FLAT, lambda o: panel_to(o).start())
-    pl.semaphore_wait(ready, spans[2] - 1)
-    each(TALL, lambda o: panel_to(o).start())
-
     put_mine(0)
+    pl.semaphore_wait(barrier, spans[0] * spans[1] * spans[2] - 1)
+    each(FLAT, lambda o: main_send_to(0, o).start())
+    each(PANELS, lambda o: panel_to(o).start())
 
     begin = pitch + 1
     chunk = 16
@@ -452,6 +446,15 @@
             each(SIDES, lambda o: strip_to(t - 1, o).wait_send())
 
 
+def put_out(force_ref, energy_ref, force_hbm, energy_hbm, sem):
+    copies = [pltpu.make_async_copy(force_ref, force_hbm, sem.at[0]),
+              pltpu.make_async_copy(energy_ref, energy_hbm, sem.at[1])]
+    for copy in copies:
+        copy.start()
+    for copy in copies:
+        copy.wait()
+
+
 def solution(mesh):
     counts = tuple(mesh.shape[axis] for axis in AXES)
 
@@ -463,7 +466,7 @@
         rows = up(2 * (pitch + 1) + up((cx + 2) * pitch + cy + 3 - (pitch + 1)))
         f32 = jnp.float32
         vmem = pl.BlockSpec(memory_space=pltpu.VMEM)
-        return pl.pallas_call(
+        force, energy = pl.pallas_call(
             functools.partial(kernel, sizes, counts),
             out_shape=(pltpu.VMEM((3,) + sizes, f32), pltpu.VMEM(sizes, f32)),
             in_specs=[pl.BlockSpec(memory_space=pl.ANY)] * 3,
@@ -498,10 +501,17 @@
                 pltpu.SemaphoreType.DMA((ITERS - 1, 2)),
                 pltpu.SemaphoreType.DMA((ITERS - 1, 2)),
                 pltpu.SemaphoreType.DMA((3,)),
-                pltpu.SemaphoreType.REGULAR,
             ],
             compiler_params=pltpu.CompilerParams(collective_id=0, has_side_effects=True),
         )(displace, occupied, strength)
+        return pl.pallas_call(
+            put_out,
+            out_shape=(jax.ShapeDtypeStruct((3,) + sizes, f32), jax.ShapeDtypeStruct(sizes, f32)),
+            in_specs=[vmem, vmem],
+            out_specs=(pl.BlockSpec(memory_space=pl.ANY),) * 2,
+            scratch_shapes=[pltpu.SemaphoreType.DMA((2,))],
+        )(pltpu.with_memory_space_constraint(force, pltpu.VMEM),
+          pltpu.with_memory_space_constraint(energy, pltpu.VMEM))
 
     in_specs = (P(None, "gx", "gy", "gz"), P("gx", "gy", "gz"), P("gx", "gy", "gz"))
     out_specs = (P(None, "gx", "gy", "gz"), P("gx", "gy", "gz"))

time: 19.4 us -> 17.9 us (0.923)
  local copies, waits for them, and re-layouts: 1.21 us -> 0 us
  Pallas kernels: 17.4 us -> 17.1 us
    unnamed x2 -> x0, local copies, waits for them, and re-layouts: 1.21 us -> none
    pallas_call x1, Pallas kernels: 17.4 us -> 16.5 us  [body(): pl.pallas_call(functools.partial(kernel, sizes, counts), out_shape=(pltpu...]
    pallas_call x0 -> x1, Pallas kernels: none -> 0.63 us  [body(): pl.pallas_call(put_out, out_shape=(jax.ShapeDtypeStruct((3,) + sizes, f32...]
where the time goes in v2:
time: 17.9 us; the launch traced here: 17.8 us
  Pallas kernels  17.1 us (96%)
  between operations  0.64 us (4%)
    pallas_call x1, Pallas kernels, body(): pl.pallas_call(functools.partial(kernel, sizes, counts), out_shape=(pltpu...  16.5 us
    pallas_call x1, Pallas kernels, body(): pl.pallas_call(put_out, out_shape=(jax.ShapeDtypeStruct((3,) + sizes, f32...  0.63 us

profile of v2, /device:TPU:1, one launch (start us, length us, event | category | flops | bytes accessed | tf_op | source)
XLA Modules:
  0.0 17.8 jit_solution(13130984600498335336)
XLA Ops:
  0.6 16.5 %shard_map.50 = (f32[3,2,8,128]{3,2,1,0:T(8,128)S(1)}, f32[2,8,128]{2,1,0:T(8,128)S(1)}) custom-call(f32[3,2,8,128]{3,2,1,0:T(8,128)} %disp_hbm.1, s32[2,8,128]{2,1,0:T(8,128)} %occ_hbm.1, f32[2,8,128]{2,1,0:T(8,128)} %str_hbm.1), custom_call_target="tpu_custom_call" | custom-call | tf_op jit(solution)/shard_map/pallas_call | solution.py:469
  17.1 0.6 %shard_map.51 = (f32[3,2,8,128]{3,2,1,0:T(8,128)}, f32[2,8,128]{2,1,0:T(8,128)}) custom-call(f32[3,2,8,128]{3,2,1,0:T(8,128)S(1)} %get-tuple-element.4.force_ref, f32[2,8,128]{2,1,0:T(8,128)S(1)} %get-tuple-element.5.energy_ref), custom_call_target="tpu_custom_call" | custom-call | tf_op jit(solution)/shard_map/pallas_call | solution.py:507

commit v3 on v2

--- a/solution.py
+++ b/solution.py
@@ -17,7 +17,7 @@
 DEEP = 2 * ITERS
 PLANE = [(dx, dy) for dx in (-1, 0, 1) for dy in (-1, 0, 1)]
 FLAT = sorted(((dx, dy, 0) for dx, dy in PLANE if (dx, dy) != (0, 0)),
-              key=lambda o: (-sum(abs(a) for a in o), o))
+              key=lambda o: (-abs(o[1]), abs(o[0]), o))
 TALL = sorted(((dx, dy, dz) for dx, dy in PLANE for dz in (-1, 1)),
               key=lambda o: (-sum(abs(a) for a in o), o))
 PANELS = TALL + FLAT
@@ -96,6 +96,7 @@
 def kernel(sizes, counts, disp_hbm, occ_hbm, str_hbm, force_ref, energy_ref,
            disp_ref, occ_ref, str_ref, xs, ys, xl, yl, near, slopes, scaled,
            stage, ps, px, pz, sp, sn, ss, sscaled, sroot, xp, xq, final,
+           zero, sink_xl, sink_yl, sink_px, sink_pz, sink_xq, tally,
            main_send, main_recv, panel_send, panel_recv, strip_send, strip_recv, load_sem):
     cx, cy, cz = sizes
     pitch = cy + 4
@@ -103,11 +104,13 @@
     group = cx * wide
     f32 = jnp.float32
 
-    loads = [pltpu.make_async_copy(disp_hbm, disp_ref, load_sem.at[0]),
-             pltpu.make_async_copy(occ_hbm, occ_ref, load_sem.at[1]),
-             pltpu.make_async_copy(str_hbm, str_ref, load_sem.at[2])]
-    for load in loads:
-        load.start()
+    for src, dst in ((disp_hbm, disp_ref), (occ_hbm, occ_ref), (str_hbm, str_ref)):
+        pltpu.make_async_copy(src, dst, load_sem).start()
+    zero[...] = jnp.zeros(zero.shape, f32)
+
+    def settle(rows, sem):
+        part = tally.at[pl.ds(0, rows)]
+        pltpu.make_async_copy(part, part, sem).wait()
 
     me = [lax.axis_index(axis) for axis in AXES]
     there = [[None if s == 0 else (m + s >= 0) & (m + s < n) for s in (-1, 0, 1)]
@@ -128,94 +131,58 @@
     spans = [1 + (m > 0).astype(jnp.int32) + (m < n - 1).astype(jnp.int32)
              for m, n in zip(me, counts)]
 
-    for s in (-1, 1):
-        @pl.when(jnp.logical_not(there[0][s + 1]))
-        def _(s=s):
-            xl[:, low(s)] = jnp.zeros(xl.shape[:1] + xl.shape[2:], f32)
-            yl[:, s + 1] = jnp.zeros(yl.shape[:1] + yl.shape[2:], f32)
-            xq[:, low(s)] = jnp.zeros(xq.shape[:1] + xq.shape[2:], f32)
-            px[3 * (s + 1):3 * (s + 1) + 3] = jnp.zeros((3,) + px.shape[1:], f32)
-            pz[3 * (s + 1):3 * (s + 1) + 3] = jnp.zeros((3,) + pz.shape[1:], f32)
-
-        @pl.when(jnp.logical_not(there[1][s + 1]))
-        def _(s=s):
-            yl[:, :, low(s)] = jnp.zeros(yl.shape[:2] + yl.shape[3:], f32)
-            for dx in range(3):
-                px[3 * dx + s + 1] = jnp.zeros(px.shape[1:], f32)
-                pz[3 * dx + s + 1] = jnp.zeros(pz.shape[1:], f32)
-
-        @pl.when(jnp.logical_not(there[2][s + 1]))
-        def _(s=s):
-            pz[:, low(s)] = jnp.zeros(pz.shape[:1] + pz.shape[2:], f32)
-
-    stage[...] = jnp.zeros(stage.shape, f32)
-    near[...] = jnp.zeros(near.shape, f32)
-    sn[...] = jnp.zeros(sn.shape, f32)
-    ss[...] = jnp.zeros(ss.shape, f32)
-
     def main_rows(t, face):
         return (4 if t == 0 else 3) * cx * cy if face else up((4 if t == 0 else 3) * cx * 2)
 
-    def main_send_to(t, o):
-        back = minus(o)
-        rows = pl.ds(0, main_rows(t, o[1] == 0))
-        if o[1] == 0:
-            src, dst = xs.at[t, rows], xl.at[t, low(back[0]), rows]
-        else:
-            src, dst = ys.at[t, low(back[1]), rows], yl.at[t, back[0] + 1, low(back[1]), rows]
-        return pltpu.make_async_remote_copy(
-            src_ref=src, dst_ref=dst, send_sem=main_send.at[t, FLAT.index(o)],
-            recv_sem=main_recv.at[t, FLAT.index(back)], device_id=target(o), device_id_type=MESH)
-
-    def main_from(t, o):
-        rows = pl.ds(0, main_rows(t, o[1] == 0))
-        spot = xl.at[t, low(o[0]), rows] if o[1] == 0 else yl.at[t, o[0] + 1, low(o[1]), rows]
-        return pltpu.make_async_remote_copy(
-            src_ref=spot, dst_ref=spot, send_sem=main_send.at[t, FLAT.index(o)],
-            recv_sem=main_recv.at[t, FLAT.index(o)], device_id=target(o), device_id_type=MESH)
-
-    def panel_spot(o):
-        j = PLANE.index(o[:2])
-        return px.at[j] if o[2] == 0 else pz.at[j, low(o[2])]
-
-    def panel_to(o):
-        back = minus(o)
-        rows = pl.ds(0, 32) if o[2] == 0 else pl.ds(8 if o[2] == -1 else 16, 16)
-        return pltpu.make_async_remote_copy(
-            src_ref=ps.at[back[1] + 1, rows], dst_ref=panel_spot(back),
-            send_sem=panel_send.at[PANELS.index(o)], recv_sem=panel_recv.at[PANELS.index(back)],
-            device_id=target(o), device_id_type=MESH)
-
-    def panel_from(o):
-        return pltpu.make_async_remote_copy(
-            src_ref=panel_spot(o), dst_ref=panel_spot(o),
-            send_sem=panel_send.at[PANELS.index(o)], recv_sem=panel_recv.at[PANELS.index(o)],
-            device_id=target(o), device_id_type=MESH)
-
-    def strip_to(t, o):
-        back = minus(o)
-        return pltpu.make_async_remote_copy(
-            src_ref=xp.at[t], dst_ref=xq.at[t, low(back[0])],
-            send_sem=strip_send.at[t, low(o[0])], recv_sem=strip_recv.at[t, low(back[0])],
-            device_id=target(o), device_id_type=MESH)
-
-    def strip_from(t, o):
-        spot = xq.at[t, low(o[0])]
-        return pltpu.make_async_remote_copy(
-            src_ref=spot, dst_ref=spot,
-            send_sem=strip_send.at[t, low(o[0])], recv_sem=strip_recv.at[t, low(o[0])],
-            device_id=target(o), device_id_type=MESH)
-
-    def each(offsets, act):
-        for o in offsets:
-            @pl.when(exists(o))
-            def _(o=o):
-                act(o)
+    def transfer(o, src, spot, sink, send_sem, recv_sem):
+        @pl.when(exists(o))
+        def _():
+            pltpu.make_async_remote_copy(
+                src_ref=src, dst_ref=spot(minus(o)), send_sem=send_sem, recv_sem=recv_sem,
+                device_id=target(o), device_id_type=MESH).start()
+
+        @pl.when(jnp.logical_not(exists(o)))
+        def _():
+            blank = zero.at[pl.ds(0, src.shape[0])]
+            pltpu.make_async_copy(blank, spot(o), recv_sem).start()
+            pltpu.make_async_copy(blank, sink(o), send_sem).start()
+
+    def main_start(t):
+        for o in FLAT:
+            rows = pl.ds(0, main_rows(t, o[1] == 0))
+            if o[1] == 0:
+                transfer(o, xs.at[t, rows], lambda n: xl.at[t, low(n[0]), rows],
+                         lambda n: sink_xl.at[low(n[0]), rows], main_send, main_recv.at[t % 2])
+            else:
+                transfer(o, ys.at[t, low(-o[1]), rows],
+                         lambda n: yl.at[t, n[0] + 1, low(n[1]), rows],
+                         lambda n: sink_yl.at[n[0] + 1, low(n[1]), rows],
+                         main_send, main_recv.at[t % 2])
+
+    def main_total(t):
+        return 2 * main_rows(t, True) + 6 * main_rows(t, False)
+
+    def panel_start():
+        for o in PANELS:
+            j = PLANE.index
+            if o[2] == 0:
+                transfer(o, ps.at[1 - o[1], pl.ds(0, 32)], lambda n: px.at[j(n[:2])],
+                         lambda n: sink_px.at[j(n[:2])], panel_send, panel_recv)
+            else:
+                transfer(o, ps.at[1 - o[1], pl.ds(8 if o[2] == -1 else 16, 16)],
+                         lambda n: pz.at[j(n[:2]), low(n[2])],
+                         lambda n: sink_pz.at[j(n[:2]), low(n[2])], panel_send, panel_recv)
+
+    panel_total = 8 * 32 + 18 * 16
+
+    def strip_start(t):
+        for o in SIDES:
+            transfer(o, xp.at[t], lambda n: xq.at[t, low(n[0])],
+                     lambda n: sink_xq.at[low(n[0])], strip_send, strip_recv.at[t])
 
     SIDES = [(-1, 0, 0), (1, 0, 0)]
 
-    for load in loads:
-        load.wait()
+    settle(5 * cx * cy, load_sem)
     mine = [[disp_ref[q, x] * UNIT for x in range(cx)] for q in range(3)]
     mine.append([occ_ref[x].astype(f32) * str_ref[x] for x in range(cx)])
 
@@ -250,6 +217,14 @@
                     put(q, row + 2 + cy, yl[t, dx + 1, 1, i * 2:i * 2 + 2])
 
     fill_sends(0)
+    pl.semaphore_wait(barrier, spans[0] * spans[1] * spans[2] - 1)
+    main_start(0)
+
+    stage[...] = jnp.zeros(stage.shape, f32)
+    tail = 3 * cx * pitch
+    near[:, :, tail:] = jnp.zeros(near.shape[:2] + (near.shape[2] - tail, LANES), f32)
+    sn[...] = jnp.zeros(sn.shape, f32)
+    ss[...] = jnp.zeros(ss.shape, f32)
 
     lane = lax.broadcasted_iota(jnp.int32, (8, LANES), 1)
     half = lax.broadcasted_iota(jnp.int32, (8, LANES), 0) < 4
@@ -272,18 +247,17 @@
         ps[1, 8 * i:8 * i + 8] = piece
         ps[0, 8 * i:8 * i + 8] = jnp.where(column < DEEP, moved(piece, -cy), 0.0)
         ps[2, 8 * i:8 * i + 8] = jnp.where(column >= DEEP + cy, moved(piece, cy), 0.0)
+    panel_start()
     put_mine(0)
-    pl.semaphore_wait(barrier, spans[0] * spans[1] * spans[2] - 1)
-    each(FLAT, lambda o: main_send_to(0, o).start())
-    each(PANELS, lambda o: panel_to(o).start())
 
     begin = pitch + 1
     chunk = 16
     extent = up((cx + 2) * pitch + cy + 3 - begin)
 
-    def main_step(t):
+    def main_density(t):
         last = t == ITERS - 1
-        each(FLAT, lambda o: main_from(t, o).wait_recv())
+        settle(main_total(t), main_recv.at[t % 2])
+        settle(main_total(t), main_send)
         put_others(t)
         if t == 0:
             weight = near[1, 3, begin:begin + extent]
@@ -305,6 +279,15 @@
             slopes[2, start:start + size] = moved(slope, -1)
             if last:
                 slopes[3, start:start + size] = total * root
+
+    def main_force(t):
+        last = t == ITERS - 1
+        outer = (lane < DEEP) | (lane >= cz - DEEP)
+
+        def merge(value, q, x):
+            start = group + x * wide + DEEP
+            return jnp.where(outer, moved(final[start:start + cy], cz - 8 - 16 * q), value)
+
         for x in range(cx):
             start = (cx + x) * pitch + 2
 
@@ -321,15 +304,15 @@
             weight = mine[3][x]
             if last:
                 for q in range(3):
-                    force_ref[q, x] = (weight * FORCE) * force[q]
-                energy_ref[x] = (weight * PAIR) * pair - jnp.where(
-                    weight > 0.0, slopes[3, start:start + cy], 0.0)
+                    force_ref[q, x] = merge((weight * FORCE) * force[q], q, x)
+                energy_ref[x] = merge((weight * PAIR) * pair - jnp.where(
+                    weight > 0.0, slopes[3, start:start + cy], 0.0), 3, x)
             else:
                 for q in range(3):
                     mine[q][x] = here[q] + (weight * (FORCE * STEP * UNIT)) * force[q]
         if not last:
             fill_sends(t + 1)
-            each(FLAT, lambda o: main_send_to(t + 1, o).start())
+            main_start(t + 1)
             put_mine(t + 1)
 
     def spread(parts, at):
@@ -344,7 +327,8 @@
     def strip_step(t):
         last = t == ITERS - 1
         if t == 0:
-            each(PANELS, lambda o: panel_from(o).wait_recv())
+            settle(panel_total, panel_recv)
+            settle(panel_total, panel_send)
 
             def flat(rows):
                 return [sum(ps[1, rows:rows + 8] if (dx, dy) == (0, 0)
@@ -367,7 +351,8 @@
                 sscaled[8 * b:8 * b + 8] = jnp.where(
                     weight > 0.0, (-0.5 / SQUARED_E) / jnp.where(weight > 0.0, weight, 1.0), 0.0)
         else:
-            each(SIDES, lambda o: strip_from(t - 1, o).wait_recv())
+            settle(64, strip_recv.at[t - 1])
+            settle(64, strip_send)
             for b in range(4):
                 for q in range(3):
                     under = moved(xq[t - 1, 0, 8 * b:8 * b + 8], -group * q)
@@ -420,30 +405,22 @@
                 new = [moved(sn[q, 4 + 8 * b:12 + 8 * b], group * (q - 1)) for q in range(3)]
                 xp[t, 8 * b:8 * b + 8] = jnp.where(
                     lane < group, new[0], jnp.where(lane < 2 * group, new[1], new[2]))
-            each(SIDES, lambda o: strip_to(t, o).start())
+            strip_start(t)
             return
         rows = []
         for q in range(4):
             rows += [results[1][q], results[0][q]]
         rows.append(jnp.zeros((LANES - 64, LANES), f32))
         final[...] = jnp.transpose(jnp.concatenate(rows, axis=0))
-        outer = (lane < DEEP) | (lane >= cz - DEEP)
-        for q in range(4):
-            for x in range(cx):
-                start = group + x * wide + DEEP
-                piece = moved(final[start:start + cy], cz - 8 - 16 * q)
-                spot = force_ref.at[q, x] if q < 3 else energy_ref.at[x]
-                spot[...] = jnp.where(outer, piece, spot[...])
 
     for t in range(ITERS):
-        main_step(t)
-        strip_step(t)
-        if t == 0:
-            each(PANELS, lambda o: panel_to(o).wait_send())
-            each(FLAT, lambda o: main_send_to(0, o).wait_send())
+        main_density(t)
+        if t < ITERS - 1:
+            main_force(t)
+            strip_step(t)
         else:
-            each(FLAT, lambda o: main_send_to(t, o).wait_send())
-            each(SIDES, lambda o: strip_to(t - 1, o).wait_send())
+            strip_step(t)
+            main_force(t)
 
 
 def put_out(force_ref, energy_ref, force_hbm, energy_hbm, sem):
@@ -494,13 +471,20 @@
                 pltpu.VMEM((ITERS - 1, 32, LANES), f32),
                 pltpu.VMEM((ITERS - 1, 2, 32, LANES), f32),
                 pltpu.VMEM((LANES, LANES), f32),
-                pltpu.SemaphoreType.DMA((ITERS, len(FLAT))),
-                pltpu.SemaphoreType.DMA((ITERS, len(FLAT))),
-                pltpu.SemaphoreType.DMA((len(PANELS),)),
-                pltpu.SemaphoreType.DMA((len(PANELS),)),
-                pltpu.SemaphoreType.DMA((ITERS - 1, 2)),
-                pltpu.SemaphoreType.DMA((ITERS - 1, 2)),
-                pltpu.SemaphoreType.DMA((3,)),
+                pltpu.VMEM((4 * cx * cy, LANES), f32),
+                pltpu.VMEM((2, 4 * cx * cy, LANES), f32),
+                pltpu.VMEM((3, 2, up(8 * cx), LANES), f32),
+                pltpu.VMEM((9, 32, LANES), f32),
+                pltpu.VMEM((9, 2, 16, LANES), f32),
+                pltpu.VMEM((2, 32, LANES), f32),
+                pltpu.VMEM((8 * 32 + 18 * 16, LANES), f32),
+                pltpu.SemaphoreType.DMA,
+                pltpu.SemaphoreType.DMA((2,)),
+                pltpu.SemaphoreType.DMA,
+                pltpu.SemaphoreType.DMA,
+                pltpu.SemaphoreType.DMA,
+                pltpu.SemaphoreType.DMA((ITERS - 1,)),
+                pltpu.SemaphoreType.DMA,
             ],
             compiler_params=pltpu.CompilerParams(collective_id=0, has_side_effects=True),
         )(displace, occupied, strength)

time: 17.9 us -> 17.1 us (0.955)
  Pallas kernels: 17.1 us -> 16.3 us
    pallas_call x1, Pallas kernels: 16.5 us -> 15.7 us  [body(): pl.pallas_call(functools.partial(kernel, sizes, counts), out_shape=(pltpu...]
where the time goes in v3:
time: 17.1 us; the launch traced here: 17 us
  Pallas kernels  16.3 us (95%)
  between operations  0.64 us (4%)
    pallas_call x1, Pallas kernels, body(): pl.pallas_call(functools.partial(kernel, sizes, counts), out_shape=(pltpu...  15.7 us
    pallas_call x1, Pallas kernels, body(): pl.pallas_call(put_out, out_shape=(jax.ShapeDtypeStruct((3,) + sizes, f32...  0.63 us

profile of v3, /device:TPU:1, one launch (start us, length us, event | category | flops | bytes accessed | tf_op | source)
XLA Modules:
  0.0 17.0 jit_solution(13865217144781757177)
XLA Ops:
  0.6 15.7 %shard_map.50 = (f32[3,2,8,128]{3,2,1,0:T(8,128)S(1)}, f32[2,8,128]{2,1,0:T(8,128)S(1)}) custom-call(f32[3,2,8,128]{3,2,1,0:T(8,128)} %disp_hbm.1, s32[2,8,128]{2,1,0:T(8,128)} %occ_hbm.1, f32[2,8,128]{2,1,0:T(8,128)} %str_hbm.1), custom_call_target="tpu_custom_call" | custom-call | tf_op jit(solution)/shard_map/pallas_call | solution.py:446
  16.3 0.6 %shard_map.51 = (f32[3,2,8,128]{3,2,1,0:T(8,128)}, f32[2,8,128]{2,1,0:T(8,128)}) custom-call(f32[3,2,8,128]{3,2,1,0:T(8,128)S(1)} %get-tuple-element.4.force_ref, f32[2,8,128]{2,1,0:T(8,128)S(1)} %get-tuple-element.5.energy_ref), custom_call_target="tpu_custom_call" | custom-call | tf_op jit(solution)/shard_map/pallas_call | solution.py:491

commit v4 on v3

--- a/solution.py
+++ b/solution.py
@@ -21,6 +21,8 @@
 TALL = sorted(((dx, dy, dz) for dx, dy in PLANE for dz in (-1, 1)),
               key=lambda o: (-sum(abs(a) for a in o), o))
 PANELS = TALL + FLAT
+AROUND = [(dx, dy, dz) for dx, dy in PLANE for dz in (-1, 0, 1) if (dx, dy, dz) != (0, 0, 0)]
+SIDES = [(-1, 0, 0), (1, 0, 0)]
 
 RADIUS = math.sqrt(RADIUS_SQ)
 UNIT = 1.0 / RADIUS
@@ -93,10 +95,43 @@
     return force, pair
 
 
+def density_and_factors(near, here, factors, last):
+    base = [[h - s * UNIT for s in (-1.0, 0.0, 1.0)] for h in here]
+    total = jnp.zeros((8, LANES), jnp.float32)
+    pair = jnp.zeros((8, LANES), jnp.float32)
+    for n, (dx, dy, dz) in enumerate(AROUND):
+        sx = near(dx, dy, dz, 0) - base[0][dx + 1]
+        sy = near(dx, dy, dz, 1) - base[1][dy + 1]
+        sz = near(dx, dy, dz, 2) - base[2][dz + 1]
+        square = sx * sx + sy * sy + sz * sz
+        inverse = lax.rsqrt(square)
+        growth = jnp.exp2(square * inverse * RATE)
+        inside = 1.0 - square
+        steep = PULL + inside * inverse
+        cut = growth * inside
+        heavy = cut * near(dx, dy, dz, 3)
+        total = total + heavy * inside
+        factors[n, 0] = heavy * steep
+        factors[n, 1] = heavy * (growth * (steep - PUSH))
+        if last:
+            pair = pair + heavy * cut
+    return total, pair
+
+
+def force_from_factors(near, slope_near, here, slope, factors):
+    base = [[h - s * UNIT for s in (-1.0, 0.0, 1.0)] for h in here]
+    force = [jnp.zeros((8, LANES), jnp.float32) for _ in range(3)]
+    for n, (dx, dy, dz) in enumerate(AROUND):
+        scale = (slope + slope_near(dx, dy, dz)) * factors[n, 0] + factors[n, 1]
+        force = [force[q] + scale * (near(dx, dy, dz, q) - base[q][d + 1])
+                 for q, d in enumerate((dx, dy, dz))]
+    return force
+
+
 def kernel(sizes, counts, disp_hbm, occ_hbm, str_hbm, force_ref, energy_ref,
            disp_ref, occ_ref, str_ref, xs, ys, xl, yl, near, slopes, scaled,
-           stage, ps, px, pz, sp, sn, ss, sscaled, sroot, xp, xq, final,
-           zero, sink_xl, sink_yl, sink_px, sink_pz, sink_xq, tally,
+           stage, ps, px, pz, sp, sn, ss, sscaled, xp, xq, final,
+           zero, sink_xl, sink_yl, sink_px, sink_pz, sink_xq, tally, factors, tails,
            main_send, main_recv, panel_send, panel_recv, strip_send, strip_recv, load_sem):
     cx, cy, cz = sizes
     pitch = cy + 4
@@ -134,53 +169,58 @@
     def main_rows(t, face):
         return (4 if t == 0 else 3) * cx * cy if face else up((4 if t == 0 else 3) * cx * 2)
 
-    def transfer(o, src, spot, sink, send_sem, recv_sem):
-        @pl.when(exists(o))
-        def _():
-            pltpu.make_async_remote_copy(
-                src_ref=src, dst_ref=spot(minus(o)), send_sem=send_sem, recv_sem=recv_sem,
-                device_id=target(o), device_id_type=MESH).start()
-
-        @pl.when(jnp.logical_not(exists(o)))
-        def _():
-            blank = zero.at[pl.ds(0, src.shape[0])]
-            pltpu.make_async_copy(blank, spot(o), recv_sem).start()
-            pltpu.make_async_copy(blank, sink(o), send_sem).start()
-
-    def main_start(t):
+    def send(plan, send_sem, recv_sem):
+        for o, src, spot, _ in plan:
+            @pl.when(exists(o))
+            def _(o=o, src=src, spot=spot):
+                pltpu.make_async_remote_copy(
+                    src_ref=src, dst_ref=spot(minus(o)), send_sem=send_sem, recv_sem=recv_sem,
+                    device_id=target(o), device_id_type=MESH).start()
+
+    def fill(plan, send_sem, recv_sem):
+        for o, src, spot, sink in plan:
+            @pl.when(jnp.logical_not(exists(o)))
+            def _(o=o, src=src, spot=spot, sink=sink):
+                blank = zero.at[pl.ds(0, src.shape[0])]
+                pltpu.make_async_copy(blank, spot(o), recv_sem).start()
+                pltpu.make_async_copy(blank, sink(o), send_sem).start()
+
+    def main_plan(t):
+        plan = []
         for o in FLAT:
             rows = pl.ds(0, main_rows(t, o[1] == 0))
             if o[1] == 0:
-                transfer(o, xs.at[t, rows], lambda n: xl.at[t, low(n[0]), rows],
-                         lambda n: sink_xl.at[low(n[0]), rows], main_send, main_recv.at[t % 2])
+                plan.append((o, xs.at[t, rows], lambda n, r=rows: xl.at[t, low(n[0]), r],
+                             lambda n, r=rows: sink_xl.at[t % 2, low(n[0]), r]))
             else:
-                transfer(o, ys.at[t, low(-o[1]), rows],
-                         lambda n: yl.at[t, n[0] + 1, low(n[1]), rows],
-                         lambda n: sink_yl.at[n[0] + 1, low(n[1]), rows],
-                         main_send, main_recv.at[t % 2])
+                plan.append((o, ys.at[t, low(-o[1]), rows],
+                             lambda n, r=rows: yl.at[t, n[0] + 1, low(n[1]), r],
+                             lambda n, r=rows: sink_yl.at[t % 2, n[0] + 1, low(n[1]), r]))
+        return plan, main_send.at[t % 2], main_recv.at[t % 2]
 
     def main_total(t):
         return 2 * main_rows(t, True) + 6 * main_rows(t, False)
 
-    def panel_start():
+    def panel_plan():
+        plan = []
         for o in PANELS:
-            j = PLANE.index
             if o[2] == 0:
-                transfer(o, ps.at[1 - o[1], pl.ds(0, 32)], lambda n: px.at[j(n[:2])],
-                         lambda n: sink_px.at[j(n[:2])], panel_send, panel_recv)
+                plan.append((o, ps.at[1 - o[1], pl.ds(0, 32)],
+                             lambda n: px.at[PLANE.index(n[:2])],
+                             lambda n: sink_px.at[PLANE.index(n[:2])]))
             else:
-                transfer(o, ps.at[1 - o[1], pl.ds(8 if o[2] == -1 else 16, 16)],
-                         lambda n: pz.at[j(n[:2]), low(n[2])],
-                         lambda n: sink_pz.at[j(n[:2]), low(n[2])], panel_send, panel_recv)
+                plan.append((o, ps.at[1 - o[1], pl.ds(8 if o[2] == -1 else 16, 16)],
+                             lambda n: pz.at[PLANE.index(n[:2]), low(n[2])],
+                             lambda n: sink_pz.at[PLANE.index(n[:2]), low(n[2])]))
+        return plan, panel_send, panel_recv
 
     panel_total = 8 * 32 + 18 * 16
 
-    def strip_start(t):
-        for o in SIDES:
-            transfer(o, xp.at[t], lambda n: xq.at[t, low(n[0])],
-                     lambda n: sink_xq.at[low(n[0])], strip_send, strip_recv.at[t])
-
-    SIDES = [(-1, 0, 0), (1, 0, 0)]
+    def strip_plan(t):
+        plan = [(o, xp.at[t], lambda n: xq.at[t, low(n[0])], lambda n: sink_xq.at[t, low(n[0])])
+                for o in SIDES]
+        return plan, strip_send.at[t], strip_recv.at[t]
+
 
     settle(5 * cx * cy, load_sem)
     mine = [[disp_ref[q, x] * UNIT for x in range(cx)] for q in range(3)]
@@ -217,10 +257,8 @@
                     put(q, row + 2 + cy, yl[t, dx + 1, 1, i * 2:i * 2 + 2])
 
     fill_sends(0)
-    pl.semaphore_wait(barrier, spans[0] * spans[1] * spans[2] - 1)
-    main_start(0)
-
     stage[...] = jnp.zeros(stage.shape, f32)
+    tails[...] = jnp.zeros(tails.shape, f32)
     tail = 3 * cx * pitch
     near[:, :, tail:] = jnp.zeros(near.shape[:2] + (near.shape[2] - tail, LANES), f32)
     sn[...] = jnp.zeros(sn.shape, f32)
@@ -247,7 +285,11 @@
         ps[1, 8 * i:8 * i + 8] = piece
         ps[0, 8 * i:8 * i + 8] = jnp.where(column < DEEP, moved(piece, -cy), 0.0)
         ps[2, 8 * i:8 * i + 8] = jnp.where(column >= DEEP + cy, moved(piece, cy), 0.0)
-    panel_start()
+    for plan in (main_plan(0), panel_plan(), main_plan(1), strip_plan(0), strip_plan(1)):
+        fill(*plan)
+    pl.semaphore_wait(barrier, spans[0] * spans[1] * spans[2] - 1)
+    send(*main_plan(0))
+    send(*panel_plan())
     put_mine(0)
 
     begin = pitch + 1
@@ -257,7 +299,7 @@
     def main_density(t):
         last = t == ITERS - 1
         settle(main_total(t), main_recv.at[t % 2])
-        settle(main_total(t), main_send)
+        settle(main_total(t), main_send.at[t % 2])
         put_others(t)
         if t == 0:
             weight = near[1, 3, begin:begin + extent]
@@ -312,7 +354,7 @@
                     mine[q][x] = here[q] + (weight * (FORCE * STEP * UNIT)) * force[q]
         if not last:
             fill_sends(t + 1)
-            main_start(t + 1)
+            send(*main_plan(t + 1))
             put_mine(t + 1)
 
     def spread(parts, at):
@@ -352,7 +394,7 @@
                     weight > 0.0, (-0.5 / SQUARED_E) / jnp.where(weight > 0.0, weight, 1.0), 0.0)
         else:
             settle(64, strip_recv.at[t - 1])
-            settle(64, strip_send)
+            settle(64, strip_send.at[t - 1])
             for b in range(4):
                 for q in range(3):
                     under = moved(xq[t - 1, 0, 8 * b:8 * b + 8], -group * q)
@@ -365,25 +407,22 @@
         starts = []
         for base in (8, 32 - DEEP):
             starts += sorted({base - reach - 1, base + DEEP + reach + 1 - 8})
-        for row in starts:
+        pairs = []
+        for n, row in enumerate(starts):
             def around(dx, dy, dz, q, row=row):
                 return sp[PLANE.index((dx, dy)), q, row + dz:row + dz + 8]
 
-            total = 1.0 + SQUARED_E * density_sum(
-                around, [sp[4, q, row:row + 8] for q in range(3)], 8)
+            total, pair = density_and_factors(
+                around, [sp[4, q, row:row + 8] for q in range(3)], factors.at[n], last)
+            total = 1.0 + SQUARED_E * total
             root = lax.rsqrt(total)
             slope = sscaled[row:row + 8] * root
             for j, (dx, dy) in enumerate(PLANE):
                 ss[j, row:row + 8] = moved(slope, -(dx * wide + dy))
+            weight = sp[4, 3, row:row + 8]
             if last:
-                sroot[row:row + 8] = total * root
-        starts = [8, 24]
-        if not last:
-            starts = []
-            for base in (8, 32 - DEEP):
-                starts += sorted({base - reach, base + DEEP + reach - 8})
-        results = []
-        for row in starts:
+                pairs.append((weight * PAIR) * pair - jnp.where(weight > 0.0, total * root, 0.0))
+        for n, row in enumerate(starts):
             def around(dx, dy, dz, q, row=row):
                 return sp[PLANE.index((dx, dy)), q, row + dz:row + dz + 8]
 
@@ -391,12 +430,11 @@
                 return ss[PLANE.index((dx, dy)), row + dz:row + dz + 8]
 
             here = [sp[4, q, row:row + 8] for q in range(3)]
-            force, pair = force_sum(around, slope_around, here, ss[4, row:row + 8], 8, last)
+            force = force_from_factors(around, slope_around, here, ss[4, row:row + 8], factors.at[n])
             weight = sp[4, 3, row:row + 8]
             if last:
-                energy = (weight * PAIR) * pair - jnp.where(
-                    weight > 0.0, sroot[row:row + 8], 0.0)
-                results.append([(weight * FORCE) * f for f in force] + [energy])
+                for q, value in enumerate([(weight * FORCE) * f for f in force] + [pairs[n]]):
+                    tails[q, n, n:n + 8] = value
             else:
                 for q in range(3):
                     sn[q, row:row + 8] = here[q] + (weight * (FORCE * STEP * UNIT)) * force[q]
@@ -405,15 +443,17 @@
                 new = [moved(sn[q, 4 + 8 * b:12 + 8 * b], group * (q - 1)) for q in range(3)]
                 xp[t, 8 * b:8 * b + 8] = jnp.where(
                     lane < group, new[0], jnp.where(lane < 2 * group, new[1], new[2]))
-            strip_start(t)
+            send(*strip_plan(t))
             return
         rows = []
         for q in range(4):
-            rows += [results[1][q], results[0][q]]
+            rows += [tails[q, 1, 0:8], tails[q, 0, 1:9]]
         rows.append(jnp.zeros((LANES - 64, LANES), f32))
         final[...] = jnp.transpose(jnp.concatenate(rows, axis=0))
 
     for t in range(ITERS):
+        if 0 < t < ITERS - 1:
+            fill(*main_plan(t + 1))
         main_density(t)
         if t < ITERS - 1:
             main_force(t)
@@ -467,22 +507,23 @@
                 pltpu.VMEM((3, 40, LANES), f32),
                 pltpu.VMEM((9, 40, LANES), f32),
                 pltpu.VMEM((40, LANES), f32),
-                pltpu.VMEM((40, LANES), f32),
                 pltpu.VMEM((ITERS - 1, 32, LANES), f32),
                 pltpu.VMEM((ITERS - 1, 2, 32, LANES), f32),
                 pltpu.VMEM((LANES, LANES), f32),
                 pltpu.VMEM((4 * cx * cy, LANES), f32),
-                pltpu.VMEM((2, 4 * cx * cy, LANES), f32),
-                pltpu.VMEM((3, 2, up(8 * cx), LANES), f32),
+                pltpu.VMEM((2, 2, 4 * cx * cy, LANES), f32),
+                pltpu.VMEM((2, 3, 2, up(8 * cx), LANES), f32),
                 pltpu.VMEM((9, 32, LANES), f32),
                 pltpu.VMEM((9, 2, 16, LANES), f32),
-                pltpu.VMEM((2, 32, LANES), f32),
+                pltpu.VMEM((ITERS - 1, 2, 32, LANES), f32),
                 pltpu.VMEM((8 * 32 + 18 * 16, LANES), f32),
-                pltpu.SemaphoreType.DMA,
+                pltpu.VMEM((4, 26, 2, 8, LANES), f32),
+                pltpu.VMEM((4, 2, 16, LANES), f32),
+                pltpu.SemaphoreType.DMA((2,)),
                 pltpu.SemaphoreType.DMA((2,)),
                 pltpu.SemaphoreType.DMA,
                 pltpu.SemaphoreType.DMA,
-                pltpu.SemaphoreType.DMA,
+                pltpu.SemaphoreType.DMA((ITERS - 1,)),
                 pltpu.SemaphoreType.DMA((ITERS - 1,)),
                 pltpu.SemaphoreType.DMA,
             ],

time: 17.1 us -> 16.8 us (0.982)
  Pallas kernels: 16.3 us -> 16 us
    pallas_call x1, Pallas kernels: 15.7 us -> 15.4 us  [body(): pl.pallas_call(functools.partial(kernel, sizes, counts), out_shape=(pltpu...]
where the time goes in v4:
time: 16.8 us; the launch traced here: 16.7 us
  Pallas kernels  16 us (95%)
  between operations  0.64 us (4%)
    pallas_call x1, Pallas kernels, body(): pl.pallas_call(functools.partial(kernel, sizes, counts), out_shape=(pltpu...  15.4 us
    pallas_call x1, Pallas kernels, body(): pl.pallas_call(put_out, out_shape=(jax.ShapeDtypeStruct((3,) + sizes, f32...  0.63 us

profile of v4, /device:TPU:1, one launch (start us, length us, event | category | flops | bytes accessed | tf_op | source)
XLA Modules:
  0.0 16.7 jit_solution(4394365442859065689)
XLA Ops:
  0.6 15.4 %shard_map.50 = (f32[3,2,8,128]{3,2,1,0:T(8,128)S(1)}, f32[2,8,128]{2,1,0:T(8,128)S(1)}) custom-call(f32[3,2,8,128]{3,2,1,0:T(8,128)} %disp_hbm.1, s32[2,8,128]{2,1,0:T(8,128)} %occ_hbm.1, f32[2,8,128]{2,1,0:T(8,128)} %str_hbm.1), custom_call_target="tpu_custom_call" | custom-call | tf_op jit(solution)/shard_map/pallas_call | solution.py:486
  16.0 0.6 %shard_map.51 = (f32[3,2,8,128]{3,2,1,0:T(8,128)}, f32[2,8,128]{2,1,0:T(8,128)}) custom-call(f32[3,2,8,128]{3,2,1,0:T(8,128)S(1)} %get-tuple-element.4.force_ref, f32[2,8,128]{2,1,0:T(8,128)S(1)} %get-tuple-element.5.energy_ref), custom_call_target="tpu_custom_call" | custom-call | tf_op jit(solution)/shard_map/pallas_call | solution.py:532

commit v5 on v4

--- a/solution.py
+++ b/solution.py
@@ -21,6 +21,7 @@
 TALL = sorted(((dx, dy, dz) for dx, dy in PLANE for dz in (-1, 1)),
               key=lambda o: (-sum(abs(a) for a in o), o))
 PANELS = TALL + FLAT
+HALF = [(dx, dy, 1) for dx, dy in PLANE] + [(1, -1, 0), (1, 0, 0), (1, 1, 0), (0, 1, 0)]
 AROUND = [(dx, dy, dz) for dx, dy in PLANE for dz in (-1, 0, 1) if (dx, dy, dz) != (0, 0, 0)]
 SIDES = [(-1, 0, 0), (1, 0, 0)]
 
@@ -49,24 +50,6 @@
 def moved(value, amount, axis=1):
     amount %= value.shape[axis]
     return value if amount == 0 else pltpu.roll(value, amount, axis)
-
-
-def density_sum(near, here, size):
-    base = [[h - s * UNIT for s in (-1.0, 0.0, 1.0)] for h in here]
-    total = jnp.zeros((size, LANES), jnp.float32)
-    for dx, dy in PLANE:
-        for dz in (-1, 0, 1):
-            if (dx, dy, dz) == (0, 0, 0):
-                continue
-            sx = near(dx, dy, dz, 0) - base[0][dx + 1]
-            sy = near(dx, dy, dz, 1) - base[1][dy + 1]
-            sz = near(dx, dy, dz, 2) - base[2][dz + 1]
-            square = sx * sx + sy * sy + sz * sz
-            distance = square * lax.rsqrt(square)
-            inside = 1.0 - square
-            total = total + near(dx, dy, dz, 3) * (
-                jnp.exp2(distance * RATE) * (inside * inside))
-    return total
 
 
 def force_sum(near, slope_near, here, slope, size, last):
@@ -129,7 +112,7 @@
 
 
 def kernel(sizes, counts, disp_hbm, occ_hbm, str_hbm, force_ref, energy_ref,
-           disp_ref, occ_ref, str_ref, xs, ys, xl, yl, near, slopes, scaled,
+           disp_ref, occ_ref, str_ref, xs, ys, xl, yl, near, slopes, scaled, halves,
            stage, ps, px, pz, sp, sn, ss, sscaled, xp, xq, final,
            zero, sink_xl, sink_yl, sink_px, sink_pz, sink_xq, tally, factors, tails,
            main_send, main_recv, panel_send, panel_recv, strip_send, strip_recv, load_sem):
@@ -257,6 +240,9 @@
                     put(q, row + 2 + cy, yl[t, dx + 1, 1, i * 2:i * 2 + 2])
 
     fill_sends(0)
+    pl.semaphore_wait(barrier, spans[0] * spans[1] * spans[2] - 1)
+    send(*main_plan(0))
+    fill(*main_plan(0))
     stage[...] = jnp.zeros(stage.shape, f32)
     tails[...] = jnp.zeros(tails.shape, f32)
     tail = 3 * cx * pitch
@@ -285,19 +271,15 @@
         ps[1, 8 * i:8 * i + 8] = piece
         ps[0, 8 * i:8 * i + 8] = jnp.where(column < DEEP, moved(piece, -cy), 0.0)
         ps[2, 8 * i:8 * i + 8] = jnp.where(column >= DEEP + cy, moved(piece, cy), 0.0)
-    for plan in (main_plan(0), panel_plan(), main_plan(1), strip_plan(0), strip_plan(1)):
-        fill(*plan)
-    pl.semaphore_wait(barrier, spans[0] * spans[1] * spans[2] - 1)
-    send(*main_plan(0))
     send(*panel_plan())
+    fill(*panel_plan())
     put_mine(0)
+    fill(*main_plan(1))
 
     begin = pitch + 1
-    chunk = 16
     extent = up((cx + 2) * pitch + cy + 3 - begin)
 
-    def main_density(t):
-        last = t == ITERS - 1
+    def main_arrive(t):
         settle(main_total(t), main_recv.at[t % 2])
         settle(main_total(t), main_send.at[t % 2])
         put_others(t)
@@ -305,32 +287,50 @@
             weight = near[1, 3, begin:begin + extent]
             scaled[begin:begin + extent] = jnp.where(
                 weight > 0.0, (-0.5 / SQUARED_E) / jnp.where(weight > 0.0, weight, 1.0), 0.0)
-        for start in range(begin, begin + extent, chunk):
-            size = min(chunk, begin + extent - start)
-
-            def around(dx, dy, dz, q, start=start, size=size):
-                row = start + dx * pitch + dy
-                return near[dz + 1, q, row:row + size]
-
-            total = 1.0 + SQUARED_E * density_sum(
-                around, [near[1, q, start:start + size] for q in range(3)], size)
+
+    last_row = begin + (cx + 2) * pitch - 3
+
+    def pair_values(n):
+        dx, dy, dz = HALF[n]
+        shift = dx * pitch + dy
+        for start in range(begin - max(shift, 0), last_row + 1 - min(shift, 0), 8):
+            parts = []
+            for q, d in enumerate((dx, dy, dz)):
+                far = near[dz + 1, q, start + shift:start + shift + 8]
+                parts.append(far - (near[1, q, start:start + 8] - d * UNIT))
+            square = parts[0] * parts[0] + parts[1] * parts[1] + parts[2] * parts[2]
+            inside = 1.0 - square
+            halves[n, start:start + 8] = jnp.exp2(square * lax.rsqrt(square) * RATE) * (inside * inside)
+
+    def main_density(t):
+        last = t == ITERS - 1
+        for n in range(len(HALF)):
+            pair_values(n)
+        for start in range(begin, last_row + 1, 8):
+            total = jnp.zeros((8, LANES), f32)
+            behind = jnp.zeros((8, LANES), f32)
+            for n, (dx, dy, dz) in enumerate(HALF):
+                to = start + dx * pitch + dy
+                back = start - dx * pitch - dy
+                total = total + near[dz + 1, 3, to:to + 8] * halves[n, start:start + 8]
+                reaction = near[1, 3, back:back + 8] * halves[n, back:back + 8]
+                if dz == 0:
+                    total = total + reaction
+                else:
+                    behind = behind + reaction
+            total = 1.0 + SQUARED_E * (total + moved(behind, 1))
             root = lax.rsqrt(total)
-            slope = scaled[start:start + size] * root
-            slopes[0, start:start + size] = moved(slope, 1)
-            slopes[1, start:start + size] = slope
-            slopes[2, start:start + size] = moved(slope, -1)
+            slope = scaled[start:start + 8] * root
+            slopes[0, start:start + 8] = moved(slope, 1)
+            slopes[1, start:start + 8] = slope
+            slopes[2, start:start + 8] = moved(slope, -1)
             if last:
-                slopes[3, start:start + size] = total * root
-
-    def main_force(t):
+                slopes[3, start:start + 8] = total * root
+
+    def main_force(t, slabs):
         last = t == ITERS - 1
-        outer = (lane < DEEP) | (lane >= cz - DEEP)
-
-        def merge(value, q, x):
-            start = group + x * wide + DEEP
-            return jnp.where(outer, moved(final[start:start + cy], cz - 8 - 16 * q), value)
-
-        for x in range(cx):
+        values = []
+        for x in slabs:
             start = (cx + x) * pitch + 2
 
             def around(dx, dy, dz, q, start=start):
@@ -345,17 +345,25 @@
             force, pair = force_sum(around, slope_around, here, slopes[1, start:start + cy], cy, last)
             weight = mine[3][x]
             if last:
-                for q in range(3):
-                    force_ref[q, x] = merge((weight * FORCE) * force[q], q, x)
-                energy_ref[x] = merge((weight * PAIR) * pair - jnp.where(
-                    weight > 0.0, slopes[3, start:start + cy], 0.0), 3, x)
+                values.append([(weight * FORCE) * f for f in force] + [
+                    (weight * PAIR) * pair - jnp.where(weight > 0.0, slopes[3, start:start + cy], 0.0)])
             else:
                 for q in range(3):
                     mine[q][x] = here[q] + (weight * (FORCE * STEP * UNIT)) * force[q]
-        if not last:
-            fill_sends(t + 1)
-            send(*main_plan(t + 1))
-            put_mine(t + 1)
+        return values
+
+    def main_send_next(t):
+        fill_sends(t + 1)
+        send(*main_plan(t + 1))
+        put_mine(t + 1)
+
+    def merge(values):
+        outer = (lane < DEEP) | (lane >= cz - DEEP)
+        for x in range(cx):
+            start = group + x * wide + DEEP
+            for q in range(4):
+                spot = force_ref.at[q, x] if q < 3 else energy_ref.at[x]
+                spot[...] = jnp.where(outer, moved(final[start:start + cy], cz - 8 - 16 * q), values[x][q])
 
     def spread(parts, at):
         found = [moved(parts[i], group * (i - at)) for i in range(3)]
@@ -366,8 +374,7 @@
         for j, (dx, dy) in enumerate(PLANE):
             sp[j, q, row:row + 8] = moved(value, -(dx * wide + dy))
 
-    def strip_step(t):
-        last = t == ITERS - 1
+    def strip_arrive(t):
         if t == 0:
             settle(panel_total, panel_recv)
             settle(panel_total, panel_send)
@@ -403,6 +410,9 @@
                         lane < 2 * group, sn[q, 4 + 8 * b:12 + 8 * b],
                         jnp.where(lane < 3 * group, over, 0.0))))
 
+
+    def strip_density(t):
+        last = t == ITERS - 1
         reach = 2 * (ITERS - 1 - t)
         starts = []
         for base in (8, 32 - DEEP):
@@ -422,6 +432,10 @@
             weight = sp[4, 3, row:row + 8]
             if last:
                 pairs.append((weight * PAIR) * pair - jnp.where(weight > 0.0, total * root, 0.0))
+        return starts, pairs
+
+    def strip_force(t, starts, pairs):
+        last = t == ITERS - 1
         for n, row in enumerate(starts):
             def around(dx, dy, dz, q, row=row):
                 return sp[PLANE.index((dx, dy)), q, row + dz:row + dz + 8]
@@ -452,15 +466,23 @@
         final[...] = jnp.transpose(jnp.concatenate(rows, axis=0))
 
     for t in range(ITERS):
-        if 0 < t < ITERS - 1:
-            fill(*main_plan(t + 1))
-        main_density(t)
+        main_arrive(t)
         if t < ITERS - 1:
-            main_force(t)
-            strip_step(t)
+            main_density(t)
+            main_force(t, range(cx))
+            main_send_next(t)
+            strip_arrive(t)
+            strip_force(t, *strip_density(t))
+            fill(*strip_plan(t))
+            if t + 2 < ITERS:
+                fill(*main_plan(t + 2))
         else:
-            strip_step(t)
-            main_force(t)
+            main_density(t)
+            strip_arrive(t)
+            strips = strip_density(t)
+            values = main_force(t, [0])
+            strip_force(t, *strips)
+            merge(values + main_force(t, range(1, cx)))
 
 
 def put_out(force_ref, energy_ref, force_hbm, energy_hbm, sem):
@@ -499,6 +521,7 @@
                 pltpu.VMEM((3, 4, rows, LANES), f32),
                 pltpu.VMEM((4, rows, LANES), f32),
                 pltpu.VMEM((rows, LANES), f32),
+                pltpu.VMEM((len(HALF), rows, LANES), f32),
                 pltpu.VMEM((2, LANES, LANES), f32),
                 pltpu.VMEM((3, 32, LANES), f32),
                 pltpu.VMEM((9, 32, LANES), f32),

time: 16.8 us -> 16.7 us (level)
  no operation moved by 1% of the time
where the time goes in v5:
time: 16.7 us; the launch traced here: 16.5 us
  Pallas kernels  15.9 us (95%)
  between operations  0.64 us (4%)
    pallas_call x1, Pallas kernels, body(): pl.pallas_call(functools.partial(kernel, sizes, counts), out_shape=(pltpu...  15.2 us
    pallas_call x1, Pallas kernels, body(): pl.pallas_call(put_out, out_shape=(jax.ShapeDtypeStruct((3,) + sizes, f32...  0.63 us

profile of v5, /device:TPU:1, one launch (start us, length us, event | category | flops | bytes accessed | tf_op | source)
XLA Modules:
  0.0 16.5 jit_solution(2916369133710504003)
XLA Ops:
  0.6 15.2 %shard_map.50 = (f32[3,2,8,128]{3,2,1,0:T(8,128)S(1)}, f32[2,8,128]{2,1,0:T(8,128)S(1)}) custom-call(f32[3,2,8,128]{3,2,1,0:T(8,128)} %disp_hbm.1, s32[2,8,128]{2,1,0:T(8,128)} %occ_hbm.1, f32[2,8,128]{2,1,0:T(8,128)} %str_hbm.1), custom_call_target="tpu_custom_call" | custom-call | tf_op jit(solution)/shard_map/pallas_call | solution.py:508
  15.9 0.6 %shard_map.51 = (f32[3,2,8,128]{3,2,1,0:T(8,128)}, f32[2,8,128]{2,1,0:T(8,128)}) custom-call(f32[3,2,8,128]{3,2,1,0:T(8,128)S(1)} %get-tuple-element.4.force_ref, f32[2,8,128]{2,1,0:T(8,128)S(1)} %get-tuple-element.5.energy_ref), custom_call_target="tpu_custom_call" | custom-call | tf_op jit(solution)/shard_map/pallas_call | solution.py:555

commit v6 on v5

--- a/solution.py
+++ b/solution.py
@@ -50,32 +50,6 @@
 def moved(value, amount, axis=1):
     amount %= value.shape[axis]
     return value if amount == 0 else pltpu.roll(value, amount, axis)
-
-
-def force_sum(near, slope_near, here, slope, size, last):
-    base = [[h - s * UNIT for s in (-1.0, 0.0, 1.0)] for h in here]
-    force = [jnp.zeros((size, LANES), jnp.float32) for _ in range(3)]
-    pair = jnp.zeros((size, LANES), jnp.float32)
-    for dx, dy in PLANE:
-        for dz in (-1, 0, 1):
-            if (dx, dy, dz) == (0, 0, 0):
-                continue
-            sx = near(dx, dy, dz, 0) - base[0][dx + 1]
-            sy = near(dx, dy, dz, 1) - base[1][dy + 1]
-            sz = near(dx, dy, dz, 2) - base[2][dz + 1]
-            weight = near(dx, dy, dz, 3)
-            square = sx * sx + sy * sy + sz * sz
-            inverse = lax.rsqrt(square)
-            growth = jnp.exp2(square * inverse * RATE)
-            inside = 1.0 - square
-            steep = PULL + inside * inverse
-            both = slope + slope_near(dx, dy, dz)
-            cut = growth * inside
-            scale = (both * steep + growth * (steep - PUSH)) * cut * weight
-            force = [force[0] + scale * sx, force[1] + scale * sy, force[2] + scale * sz]
-            if last:
-                pair = pair + weight * (cut * cut)
-    return force, pair
 
 
 def density_and_factors(near, here, factors, last):
@@ -112,7 +86,7 @@
 
 
 def kernel(sizes, counts, disp_hbm, occ_hbm, str_hbm, force_ref, energy_ref,
-           disp_ref, occ_ref, str_ref, xs, ys, xl, yl, near, slopes, scaled, halves,
+           disp_ref, occ_ref, str_ref, xs, ys, xl, yl, near, slopes, scaled, halves, bonds,
            stage, ps, px, pz, sp, sn, ss, sscaled, xp, xq, final,
            zero, sink_xl, sink_yl, sink_px, sink_pz, sink_xq, tally, factors, tails,
            main_send, main_recv, panel_send, panel_recv, strip_send, strip_recv, load_sem):
@@ -240,15 +214,7 @@
                     put(q, row + 2 + cy, yl[t, dx + 1, 1, i * 2:i * 2 + 2])
 
     fill_sends(0)
-    pl.semaphore_wait(barrier, spans[0] * spans[1] * spans[2] - 1)
-    send(*main_plan(0))
-    fill(*main_plan(0))
     stage[...] = jnp.zeros(stage.shape, f32)
-    tails[...] = jnp.zeros(tails.shape, f32)
-    tail = 3 * cx * pitch
-    near[:, :, tail:] = jnp.zeros(near.shape[:2] + (near.shape[2] - tail, LANES), f32)
-    sn[...] = jnp.zeros(sn.shape, f32)
-    ss[...] = jnp.zeros(ss.shape, f32)
 
     lane = lax.broadcasted_iota(jnp.int32, (8, LANES), 1)
     half = lax.broadcasted_iota(jnp.int32, (8, LANES), 0) < 4
@@ -271,8 +237,16 @@
         ps[1, 8 * i:8 * i + 8] = piece
         ps[0, 8 * i:8 * i + 8] = jnp.where(column < DEEP, moved(piece, -cy), 0.0)
         ps[2, 8 * i:8 * i + 8] = jnp.where(column >= DEEP + cy, moved(piece, cy), 0.0)
+    pl.semaphore_wait(barrier, spans[0] * spans[1] * spans[2] - 1)
+    send(*main_plan(0))
     send(*panel_plan())
+    fill(*main_plan(0))
     fill(*panel_plan())
+    tails[...] = jnp.zeros(tails.shape, f32)
+    tail = 3 * cx * pitch
+    near[:, :, tail:] = jnp.zeros(near.shape[:2] + (near.shape[2] - tail, LANES), f32)
+    sn[...] = jnp.zeros(sn.shape, f32)
+    ss[...] = jnp.zeros(ss.shape, f32)
     put_mine(0)
     fill(*main_plan(1))
 
@@ -290,7 +264,9 @@
 
     last_row = begin + (cx + 2) * pitch - 3
 
-    def pair_values(n):
+    own_first, own_last = cx * pitch + 2, (2 * cx - 1) * pitch + 1 + cy
+
+    def pair_values(n, last):
         dx, dy, dz = HALF[n]
         shift = dx * pitch + dy
         for start in range(begin - max(shift, 0), last_row + 1 - min(shift, 0), 8):
@@ -299,13 +275,22 @@
                 far = near[dz + 1, q, start + shift:start + shift + 8]
                 parts.append(far - (near[1, q, start:start + 8] - d * UNIT))
             square = parts[0] * parts[0] + parts[1] * parts[1] + parts[2] * parts[2]
+            inverse = lax.rsqrt(square)
+            growth = jnp.exp2(square * inverse * RATE)
             inside = 1.0 - square
-            halves[n, start:start + 8] = jnp.exp2(square * lax.rsqrt(square) * RATE) * (inside * inside)
+            cut = growth * inside
+            halves[n, start:start + 8] = cut * inside
+            if start + 8 > own_first - max(shift, 0) and start <= own_last - min(shift, 0):
+                steep = PULL + inside * inverse
+                bonds[n, 0, start:start + 8] = cut * steep
+                bonds[n, 1, start:start + 8] = cut * (growth * (steep - PUSH))
+                if last:
+                    bonds[n, 2, start:start + 8] = cut * cut
 
     def main_density(t):
         last = t == ITERS - 1
         for n in range(len(HALF)):
-            pair_values(n)
+            pair_values(n, last)
         for start in range(begin, last_row + 1, 8):
             total = jnp.zeros((8, LANES), f32)
             behind = jnp.zeros((8, LANES), f32)
@@ -332,17 +317,25 @@
         values = []
         for x in slabs:
             start = (cx + x) * pitch + 2
-
-            def around(dx, dy, dz, q, start=start):
-                row = start + dx * pitch + dy
-                return near[dz + 1, q, row:row + cy]
-
-            def slope_around(dx, dy, dz, start=start):
-                row = start + dx * pitch + dy
-                return slopes[dz + 1, row:row + cy]
-
             here = [mine[q][x] for q in range(3)]
-            force, pair = force_sum(around, slope_around, here, slopes[1, start:start + cy], cy, last)
+            base = [[h - s * UNIT for s in (-1.0, 0.0, 1.0)] for h in here]
+            slope = slopes[1, start:start + cy]
+            force = [jnp.zeros((cy, LANES), f32) for _ in range(3)]
+            pair = jnp.zeros((cy, LANES), f32)
+            for o in AROUND:
+                row = start + o[0] * pitch + o[1]
+
+                def bond(k, o=o, row=row):
+                    if o in HALF:
+                        return bonds[HALF.index(o), k, start:start + cy]
+                    return moved(bonds[HALF.index(minus(o)), k, row:row + cy], -o[2])
+
+                far = near[o[2] + 1, 3, row:row + cy]
+                scale = far * ((slope + slopes[o[2] + 1, row:row + cy]) * bond(0) + bond(1))
+                force = [force[q] + scale * (near[o[2] + 1, q, row:row + cy] - base[q][d + 1])
+                         for q, d in enumerate(o)]
+                if last:
+                    pair = pair + far * bond(2)
             weight = mine[3][x]
             if last:
                 values.append([(weight * FORCE) * f for f in force] + [
@@ -522,6 +515,7 @@
                 pltpu.VMEM((4, rows, LANES), f32),
                 pltpu.VMEM((rows, LANES), f32),
                 pltpu.VMEM((len(HALF), rows, LANES), f32),
+                pltpu.VMEM((len(HALF), 3, rows, LANES), f32),
                 pltpu.VMEM((2, LANES, LANES), f32),
                 pltpu.VMEM((3, 32, LANES), f32),
                 pltpu.VMEM((9, 32, LANES), f32),

time: 16.7 us -> 16.5 us (0.988)
  Pallas kernels: 15.9 us -> 15.7 us
where the time goes in v6:
time: 16.5 us; the launch traced here: 16.4 us
  Pallas kernels  15.7 us (95%)
  between operations  0.64 us (4%)
    pallas_call x1, Pallas kernels, body(): pl.pallas_call(functools.partial(kernel, sizes, counts), out_shape=(pltpu...  15.1 us
    pallas_call x1, Pallas kernels, body(): pl.pallas_call(put_out, out_shape=(jax.ShapeDtypeStruct((3,) + sizes, f32...  0.63 us

profile of v6, /device:TPU:1, one launch (start us, length us, event | category | flops | bytes accessed | tf_op | source)
XLA Modules:
  0.0 16.4 jit_solution(6182042361987203082)
XLA Ops:
  0.6 15.1 %shard_map.50 = (f32[3,2,8,128]{3,2,1,0:T(8,128)S(1)}, f32[2,8,128]{2,1,0:T(8,128)S(1)}) custom-call(f32[3,2,8,128]{3,2,1,0:T(8,128)} %disp_hbm.1, s32[2,8,128]{2,1,0:T(8,128)} %occ_hbm.1, f32[2,8,128]{2,1,0:T(8,128)} %str_hbm.1), custom_call_target="tpu_custom_call" | custom-call | tf_op jit(solution)/shard_map/pallas_call | solution.py:501
  15.7 0.6 %shard_map.51 = (f32[3,2,8,128]{3,2,1,0:T(8,128)}, f32[2,8,128]{2,1,0:T(8,128)}) custom-call(f32[3,2,8,128]{3,2,1,0:T(8,128)S(1)} %get-tuple-element.4.force_ref, f32[2,8,128]{2,1,0:T(8,128)S(1)} %get-tuple-element.5.energy_ref), custom_call_target="tpu_custom_call" | custom-call | tf_op jit(solution)/shard_map/pallas_call | solution.py:549

commit v7 on v6

--- a/solution.py
+++ b/solution.py
@@ -124,7 +124,7 @@
              for m, n in zip(me, counts)]
 
     def main_rows(t, face):
-        return (4 if t == 0 else 3) * cx * cy if face else up((4 if t == 0 else 3) * cx * 2)
+        return (4 if t == 0 else 3) * cx * (cy if face else 2)
 
     def send(plan, send_sem, recv_sem):
         for o, src, spot, _ in plan:
@@ -312,10 +312,9 @@
             if last:
                 slopes[3, start:start + 8] = total * root
 
-    def main_force(t, slabs):
+    def main_force(t):
         last = t == ITERS - 1
-        values = []
-        for x in slabs:
+        for x in range(cx):
             start = (cx + x) * pitch + 2
             here = [mine[q][x] for q in range(3)]
             base = [[h - s * UNIT for s in (-1.0, 0.0, 1.0)] for h in here]
@@ -338,25 +337,26 @@
                     pair = pair + far * bond(2)
             weight = mine[3][x]
             if last:
-                values.append([(weight * FORCE) * f for f in force] + [
-                    (weight * PAIR) * pair - jnp.where(weight > 0.0, slopes[3, start:start + cy], 0.0)])
+                for q in range(3):
+                    force_ref[q, x] = (weight * FORCE) * force[q]
+                energy_ref[x] = (weight * PAIR) * pair - jnp.where(
+                    weight > 0.0, slopes[3, start:start + cy], 0.0)
             else:
                 for q in range(3):
                     mine[q][x] = here[q] + (weight * (FORCE * STEP * UNIT)) * force[q]
-        return values
 
     def main_send_next(t):
         fill_sends(t + 1)
         send(*main_plan(t + 1))
         put_mine(t + 1)
 
-    def merge(values):
+    def merge():
         outer = (lane < DEEP) | (lane >= cz - DEEP)
         for x in range(cx):
             start = group + x * wide + DEEP
             for q in range(4):
                 spot = force_ref.at[q, x] if q < 3 else energy_ref.at[x]
-                spot[...] = jnp.where(outer, moved(final[start:start + cy], cz - 8 - 16 * q), values[x][q])
+                spot[...] = jnp.where(outer, moved(final[start:start + cy], cz - 8 - 16 * q), spot[...])
 
     def spread(parts, at):
         found = [moved(parts[i], group * (i - at)) for i in range(3)]
@@ -462,7 +462,7 @@
         main_arrive(t)
         if t < ITERS - 1:
             main_density(t)
-            main_force(t, range(cx))
+            main_force(t)
             main_send_next(t)
             strip_arrive(t)
             strip_force(t, *strip_density(t))
@@ -471,11 +471,10 @@
                 fill(*main_plan(t + 2))
         else:
             main_density(t)
+            main_force(t)
             strip_arrive(t)
-            strips = strip_density(t)
-            values = main_force(t, [0])
-            strip_force(t, *strips)
-            merge(values + main_force(t, range(1, cx)))
+            strip_force(t, *strip_density(t))
+            merge()
 
 
 def put_out(force_ref, energy_ref, force_hbm, energy_hbm, sem):

time: 16.5 us -> 16.5 us (level)
  no operation moved by 1% of the time
where the time goes in v7:
time: 16.5 us; the launch traced here: 16.3 us
  Pallas kernels  15.7 us (95%)
  between operations  0.64 us (4%)
    pallas_call x1, Pallas kernels, body(): pl.pallas_call(functools.partial(kernel, sizes, counts), out_shape=(pltpu...  15 us
    pallas_call x1, Pallas kernels, body(): pl.pallas_call(put_out, out_shape=(jax.ShapeDtypeStruct((3,) + sizes, f32...  0.63 us

profile of v7, /device:TPU:1, one launch (start us, length us, event | category | flops | bytes accessed | tf_op | source)
XLA Modules:
  0.0 16.3 jit_solution(17702998711489920191)
XLA Ops:
  0.6 15.0 %shard_map.50 = (f32[3,2,8,128]{3,2,1,0:T(8,128)S(1)}, f32[2,8,128]{2,1,0:T(8,128)S(1)}) custom-call(f32[3,2,8,128]{3,2,1,0:T(8,128)} %disp_hbm.1, s32[2,8,128]{2,1,0:T(8,128)} %occ_hbm.1, f32[2,8,128]{2,1,0:T(8,128)} %str_hbm.1), custom_call_target="tpu_custom_call" | custom-call | tf_op jit(solution)/shard_map/pallas_call | solution.py:500
  15.7 0.6 %shard_map.51 = (f32[3,2,8,128]{3,2,1,0:T(8,128)}, f32[2,8,128]{2,1,0:T(8,128)}) custom-call(f32[3,2,8,128]{3,2,1,0:T(8,128)S(1)} %get-tuple-element.4.force_ref, f32[2,8,128]{2,1,0:T(8,128)S(1)} %get-tuple-element.5.energy_ref), custom_call_target="tpu_custom_call" | custom-call | tf_op jit(solution)/shard_map/pallas_call | solution.py:548
